TPU v7x, 128 devices: a whole 4x4x4 slice. The times are simulated.
128 devices in a mesh: row: 8 (over z, core), col: 16 (over x, y).
Axes of the slice: x: 4, y: 4, z: 4, core: 2. Of those that a mesh axis runs over, the one named last changes fastest.
Arguments:
- hamiltonian: bfloat16 [4096, 4096], P('row', 'col'), may hold values from -0.3 to 0.3
- pattern: int32 [32, 32], replicated, may hold values from 0 to 1, as said below
- tile_lists: int32 [128, 8], replicated, may hold values from 0 to 31, as said below
- orders: int32 [128], replicated, may hold values from 6 to 8
- shift: float32 [1], replicated, may hold values from -0.5 to 0.5
Outputs:
- density: bfloat16 [4096, 4096], P('row', 'col')
- php: float32 [4096, 4096], P('row', 'col')
Inputs may be any that keep to these rules, and one draw needn't show every extreme that they name: `pattern`: Symmetric, with zeros on the diagonal. `tile_lists`: row s begins with tile s * 32 // 128; its entries lie in distinct groups of 2 consecutive tiles, and the second lies in the group that shares a group of 4 consecutive tiles with the first. Entries from position orders[s] on are not used.
All inputs are finite; a program needn't handle non-finite values.
Results may differ from a plain program's by a relative error of at most 0.0073.
Values may be sent and summed in bfloat16 or wider, within the bound.
No kernel may reach another device: no remote copies, remote signals or barrier semaphores. Data moves between devices by JAX's collectives and lax.ppermute only.
A program may use at most 64 MiB of HBM per device.

v0:
```python
import jax
import jax.numpy as jnp
from jax import lax
from jax.experimental import pallas as pl
from jax.experimental.pallas import tpu as pltpu
from jax.sharding import Mesh
from jax.sharding import PartitionSpec as P

TILE = 128
MAXT = 8
NB = 32
ROWS = 8
COLS = 16
CW = 32
N = MAXT * TILE
RT = NB // ROWS
CT = NB // COLS
WIDTH = CT * TILE
ROW = ("z", "core")
COL = ("c0", "c1")
F32 = jnp.float32
BF16 = jnp.bfloat16


def kept(pattern, a, b):
    return (pattern[a * NB + b] > 0) | (a == b)


def ring_owner(ids, k, part):
    return (ids[0] // 2 + k) % 4 * 2 + (ids[0] + part) % 2


def row_copies(ids, blocks, whole, sems):
    copies = []
    for part in range(2):
        for k in range(4):
            rows = pl.ds(pl.multiple_of(ring_owner(ids, k, part) * RT * TILE, RT * TILE), RT * TILE)
            copies.append(
                pltpu.make_async_copy(blocks[part * 4 + k], whole.at[rows, :], sems.at[part, k])
            )
    return copies


def cyclic(j, k):
    return 1 + (j - 1 + k) % (MAXT - 1)


def pack_kernel(ids, lists, orders, *refs):
    blocks, (out, first, strip, sems) = refs[:8], refs[8:]
    copies = row_copies(ids, blocks, strip, sems)
    for copy in copies:
        copy.start()
    for copy in copies:
        copy.wait()

    def tile(a, lanes):
        return strip[pl.ds(pl.multiple_of(a * TILE, TILE), TILE), lanes]

    own = (ids[1] * ROWS + ids[0]) * MAXT
    lanes = pl.ds(pl.multiple_of(lists[own] % CT * TILE, TILE), TILE)
    for i in range(MAXT):
        first[i] = tile(lists[own + i], lanes)

    def one(c, _):
        s = c * ROWS + ids[0]
        for j in range(1, MAXT):
            b = lists[s * MAXT + j]

            @pl.when((b // CT == ids[1]) & (j < orders[s]))
            def _():
                lanes = pl.ds(pl.multiple_of(b % CT * TILE, TILE), TILE)
                for k in range(4):
                    out[c, k] = tile(lists[s * MAXT + cyclic(j, k)], lanes)

        return 0

    lax.fori_loop(0, COLS, one, 0)


def solve_kernel(ids, lists, orders, pattern, shift, tiles, first, panel, x, f, y, d):
    s = ids[1] * ROWS + ids[0]
    order = orders[s]
    potential = shift[0]
    names = [lists[s * MAXT + j] for j in range(MAXT)]
    rows = lax.broadcasted_iota(jnp.int32, (TILE, TILE), 0)
    cols = lax.broadcasted_iota(jnp.int32, (TILE, TILE), 1)
    eye = jnp.where(rows == cols, 1.0, 0.0).astype(F32)

    def put(i, j, tile):
        y[pl.ds(i * TILE, TILE), pl.ds(j * TILE, TILE)] = tile

    for i in range(MAXT):
        put(i, 0, first[i])
        if i:
            put(0, i, first[i].T)
            for k in range(4):
                tile = tiles[names[i] // CT, k]
                put(cyclic(i, k), i, tile)
                if k:
                    put(i, cyclic(i, k), tile.T)

    def shifted(i, j):
        both = kept(pattern, names[i], names[j]) & (i < order) & (j < order)
        tile = y[pl.ds(i * TILE, TILE), pl.ds(j * TILE, TILE)].astype(F32)
        tile = jnp.where(both, tile, 0.0)
        if i == j:
            tile = tile - jnp.where(i < order, potential, 0.0) * eye
        return tile

    largest = jnp.zeros((), F32)
    for i in range(MAXT):
        total = jnp.zeros((TILE, TILE), F32)
        for j in range(MAXT):
            tile = shifted(i, j)
            total = total + tile * tile
        largest = jnp.maximum(largest, jnp.max(jnp.sum(total, axis=1)))
    root = jnp.sqrt(jnp.full((8, TILE), largest + 1e-06, F32))
    inverse = (1.0 / (jnp.abs(potential) + 2.0 * root))[0:1, :]
    for i in range(MAXT):
        for j in range(MAXT):
            x[pl.ds(i * TILE, TILE), pl.ds(j * TILE, TILE)] = (shifted(i, j) * inverse).astype(BF16)

    band = 512
    brow = lax.broadcasted_iota(jnp.int32, (band, N), 0)
    bcol = lax.broadcasted_iota(jnp.int32, (band, N), 1)

    def step(source, target):
        def square(b, _):
            here = pl.ds(pl.multiple_of(b * band, band), band)
            q = jnp.dot(source[here, :], source[...], preferred_element_type=F32)
            diag = jnp.where(brow + b * band == bcol, 1.5, 0.0)
            f[here, :] = (diag - 0.5 * q).astype(BF16)
            return 0

        def apply(b, _):
            here = pl.ds(pl.multiple_of(b * band, band), band)
            target[here, :] = jnp.dot(
                source[here, :], f[...], preferred_element_type=F32
            ).astype(BF16)
            return 0

        lax.fori_loop(0, N // band, square, 0)
        lax.fori_loop(0, N // band, apply, 0)

    step(x, y)
    step(y, x)
    head = pl.ds(0, TILE)
    prow = lax.broadcasted_iota(jnp.int32, (N, TILE), 0)
    pcol = lax.broadcasted_iota(jnp.int32, (N, TILE), 1)
    q = jnp.dot(x[...], x[:, head], preferred_element_type=F32)
    f[:, head] = (jnp.where(prow == pcol, 1.5, 0.0) - 0.5 * q).astype(BF16)
    z = jnp.dot(x[...], f[:, head], preferred_element_type=F32)
    dens = jnp.where(prow == pcol, 0.5, 0.0) - 0.5 * z
    for i in range(MAXT):
        d[:, pl.ds(i * TILE, TILE)] = dens[i * TILE : (i + 1) * TILE, :].T
    offset = pl.multiple_of(s % (TILE // CW) * CW, CW)
    for i in range(MAXT):
        panel[i] = d[pl.ds(offset, CW), pl.ds(i * TILE, TILE)].astype(BF16)


def spread_kernel(ids, lists, orders, panels, out, mine):
    mine[...] = jnp.zeros_like(mine)
    for k in range(ROWS):
        s = ids[1] * ROWS + k
        for i in range(MAXT):
            group = lists[s * MAXT + i] // CT

            @pl.when((i < orders[s]) & (group // (RT // CT) == ids[0]))
            def _():
                mine[k, group % (RT // CT)] = panels[k, i]

    def one(c, _):
        out[c] = mine[...]
        return 0

    lax.fori_loop(0, COLS, one, 0)


def hp_kernel(ids, lists, orders, pattern, a0, a1, a2, a3, b0, b1, b2, b3, panels, hp, pt, wide, sems):
    half = RT * TILE // 2
    c0 = ids[1] // 4
    c1 = ids[1] % 4
    copies = []
    for k in range(4):
        for m in range(4):
            first = (c0 + k) % 4 * 4 + (c1 + m) % 4
            second = (c0 + m) % 4 * 4 + (c1 + k) % 4
            for part, ref, col in ((0, (a0, a1, a2, a3)[k], first), (1, (b0, b1, b2, b3)[k], second)):
                lanes = pl.ds(pl.multiple_of(col * WIDTH, WIDTH), WIDTH)
                copies.append(
                    pltpu.make_async_copy(
                        ref.at[m], wide.at[pl.ds(part * half, half), lanes], sems.at[part, k, m]
                    )
                )
    for copy in copies:
        copy.start()
    pt[...] = jnp.zeros_like(pt)
    for k in range(ROWS):
        s = ids[1] * ROWS + k
        for i in range(MAXT):

            @pl.when(i < orders[s])
            def _():
                where = pl.multiple_of(lists[s * MAXT + i] * TILE, TILE)
                pt[pl.ds(k * CW, CW), pl.ds(where, TILE)] = panels[k, i]

    for copy in copies:
        copy.wait()

    def clear(b, _):
        lanes = pl.ds(pl.multiple_of(b * TILE, TILE), TILE)
        for a in range(RT):

            @pl.when(jnp.logical_not(kept(pattern, ids[0] * RT + a, b)))
            def _():
                wide[pl.ds(a * TILE, TILE), lanes] = jnp.zeros((TILE, TILE), BF16)

        return 0

    lax.fori_loop(0, NB, clear, 0)
    hp[...] = lax.dot_general(
        wide[...], pt[...], (((1,), (1,)), ((), ())), preferred_element_type=F32
    ).astype(BF16)


def final_kernel(ids, present, pieces, *refs):
    blocks = refs[:8]
    density, php, pt, arrived, hp, sem, sems = refs[8:]
    copies = row_copies(ids, blocks, hp, sems)
    panels = pltpu.make_async_copy(pieces, arrived, sem)
    for copy in [panels] + copies:
        copy.start()
    panels.wait()

    def place(c, _):
        for r in range(ROWS):
            s = c * ROWS + r
            here = pl.ds(pl.multiple_of(s * CW, CW), CW)
            for g in range(RT // CT):
                piece = arrived[c, r, g]
                for a in range(g * CT, g * CT + CT):
                    live = present[s * RT + a] > 0
                    pt[here, pl.ds(a * TILE, TILE)] = jnp.where(live, piece, jnp.zeros_like(piece))
        return 0

    lax.fori_loop(0, COLS, place, 0)
    for copy in copies:
        copy.wait()
    php[...] = lax.dot_general(
        pt[...], hp[...], (((0,), (0,)), ((), ())), preferred_element_type=F32
    )
    mine = pt[pl.ds(pl.multiple_of(ids[1] * WIDTH, WIDTH), WIDTH), :]
    density[...] = mine.T


def from_ring(x, axis):
    return [x] + [lax.ppermute(x, axis, [((i + k) % 4, i) for i in range(4)]) for k in range(1, 4)]


def swapped(x):
    return lax.ppermute(x, "core", [(0, 1), (1, 0)])


def steps(hamiltonian, pattern, tile_lists, orders, shift):
    row = lax.axis_index(ROW)
    col = lax.axis_index(COL)
    ids = jnp.stack([row, col]).astype(jnp.int32)
    lists = tile_lists.reshape(-1)
    smem = pl.BlockSpec(memory_space=pltpu.SMEM)
    vmem = pl.BlockSpec(memory_space=pltpu.VMEM)
    hbm = pl.BlockSpec(memory_space=pl.ANY)
    flat_pattern = pattern.reshape(-1)
    half = RT * TILE // 2
    strip = from_ring(hamiltonian, "z")
    ahead = from_ring(hamiltonian[:half], "c1")
    across = from_ring(hamiltonian[half:], "c0")
    strip = strip + [swapped(x) for x in strip]
    packed, first = pl.pallas_call(
        pack_kernel,
        out_shape=(
            jax.ShapeDtypeStruct((COLS, 4, TILE, TILE), BF16),
            jax.ShapeDtypeStruct((MAXT, TILE, TILE), BF16),
        ),
        in_specs=[smem, smem, smem] + [hbm] * 8,
        out_specs=(vmem, vmem),
        scratch_shapes=[pltpu.VMEM((NB * TILE, WIDTH), BF16), pltpu.SemaphoreType.DMA((2, 4))],
        name="pack",
    )(ids, lists, orders, *strip)
    packed, ahead, across = lax.optimization_barrier((packed, ahead, across))
    tiles = lax.all_to_all(packed, COL, 0, 0, tiled=True)
    ahead = from_ring(jnp.stack(ahead), "c0")
    across = from_ring(jnp.stack(across), "c1")
    panel = pl.pallas_call(
        solve_kernel,
        out_shape=jax.ShapeDtypeStruct((MAXT, CW, TILE), BF16),
        in_specs=[smem] * 5 + [vmem, vmem],
        out_specs=vmem,
        scratch_shapes=[
            pltpu.VMEM((N, N), BF16),
            pltpu.VMEM((N, N), BF16),
            pltpu.VMEM((N, N), BF16),
            pltpu.VMEM((TILE, N), F32),
        ],
        name="solve",
    )(ids, lists, orders, flat_pattern, shift, tiles, first)
    panels = lax.all_gather(panel, ROW, axis=0, tiled=False)
    spread = pl.pallas_call(
        spread_kernel,
        out_shape=jax.ShapeDtypeStruct((COLS, ROWS, RT // CT, CW, TILE), BF16),
        in_specs=[smem] * 3 + [vmem],
        out_specs=vmem,
        scratch_shapes=[pltpu.VMEM((ROWS, RT // CT, CW, TILE), BF16)],
        name="spread",
    )(ids, lists, orders, panels)
    arrived = lax.all_to_all(spread, COL, 0, 0, tiled=True)
    hp = pl.pallas_call(
        hp_kernel,
        out_shape=jax.ShapeDtypeStruct((RT * TILE, WIDTH), BF16),
        in_specs=[smem] * 4 + [hbm] * 8 + [vmem],
        out_specs=vmem,
        scratch_shapes=[
            pltpu.VMEM((WIDTH, NB * TILE), BF16),
            pltpu.VMEM((RT * TILE, NB * TILE), BF16),
            pltpu.SemaphoreType.DMA((2, 4, 4)),
        ],
        name="hp",
    )(ids, lists, orders, flat_pattern, *ahead, *across, panels)
    ours = from_ring(hp, "z")
    theirs = [swapped(x) for x in ours]
    own = row * RT + jnp.arange(RT, dtype=jnp.int32)
    live = jnp.arange(MAXT, dtype=jnp.int32)[None, :] < orders[:, None]
    present = jnp.any((tile_lists[:, None, :] == own[None, :, None]) & live[:, None, :], axis=2)
    density, php = pl.pallas_call(
        final_kernel,
        out_shape=(
            jax.ShapeDtypeStruct((RT * TILE, WIDTH), BF16),
            jax.ShapeDtypeStruct((RT * TILE, WIDTH), F32),
        ),
        in_specs=[smem, smem] + [hbm] * 9,
        out_specs=(vmem, vmem),
        scratch_shapes=[
            pltpu.VMEM((NB * TILE, RT * TILE), BF16),
            pltpu.VMEM((COLS, ROWS, RT // CT, CW, TILE), BF16),
            pltpu.VMEM((NB * TILE, WIDTH), BF16),
            pltpu.SemaphoreType.DMA,
            pltpu.SemaphoreType.DMA((2, 4)),
        ],
        name="final",
    )(ids, present.astype(jnp.int32).reshape(-1), arrived, *ours, *theirs)
    return density, php


def solution(mesh):
    fine = Mesh(mesh.devices.reshape(4, 2, 4, 4), ("z", "core", "c0", "c1"))
    split = P(ROW, COL)
    return jax.shard_map(
        steps,
        mesh=fine,
        in_specs=(split, P(), P(), P(), P()),
        out_specs=(split, split),
        check_vma=False,
    )
```

profile of v0, /device:TPU:1, one launch (start us, length us, event | category | flops | bytes accessed | tf_op | source)
XLA Modules:
  0.0 203.0 jit_solution(2662438721273543613)
XLA Ops:
  0.6 2.5 %collective-permute-start.2 = (bf16[512,256]{1,0:T(8,128)(2,1)}, bf16[512,256]{1,0:T(8,128)(2,1)S(1)}, u32[]{:S(2)}, u32[]{:S(2)}) collective-permute-start(bf16[512,256]{1,0:T(8,128)(2,1)} %refs_0_.1), channel_id=1, source_target_pairs={{96,0},{0,32},{32,64},{64,96},{97,1},{1,33},{33,65},{65,97},{98,2}... | collective-permute-start | bytes 786440 | tf_op jit(solution)/shard_map/ppermute | solution.py:257
  3.2 3.3 %collective-permute-start.1 = (bf16[512,256]{1,0:T(8,128)(2,1)}, bf16[512,256]{1,0:T(8,128)(2,1)S(1)}, u32[]{:S(2)}, u32[]{:S(2)}) collective-permute-start(bf16[512,256]{1,0:T(8,128)(2,1)} %refs_0_.1), channel_id=1, source_target_pairs={{64,0},{96,32},{0,64},{32,96},{65,1},{97,33},{1,65},{33,97},{66,2}... | collective-permute-start | bytes 786440 | tf_op jit(solution)/shard_map/ppermute | solution.py:257
  6.5 0.7 collective-permute-start
  7.2 1.5 collective-permute-start.3
  8.7 2.8 %collective-permute-done.2.refs_3_ = bf16[512,256]{1,0:T(8,128)(2,1)S(1)} collective-permute-done((bf16[512,256]{1,0:T(8,128)(2,1)}, bf16[512,256]{1,0:T(8,128)(2,1)S(1)}, u32[]{:S(2)}, u32[]{:S(2)}) %collective-permute-start.2) | collective-permute-done | bytes 262176 | tf_op jit(solution)/shard_map/ppermute | solution.py:257
  11.5 1.3 collective-permute-start.6
  12.7 5.3 %collective-permute-done.1.refs_2_ = bf16[512,256]{1,0:T(8,128)(2,1)S(1)} collective-permute-done((bf16[512,256]{1,0:T(8,128)(2,1)}, bf16[512,256]{1,0:T(8,128)(2,1)S(1)}, u32[]{:S(2)}, u32[]{:S(2)}) %collective-permute-start.1) | collective-permute-done | bytes 262176 | tf_op jit(solution)/shard_map/ppermute | solution.py:257
  18.0 1.5 collective-permute-start.5
  19.5 0.1 collective-permute-start.4
  19.6 1.0 fusion
  20.6 1.3 collective-permute-start.12
  21.9 4.6 %collective-permute-done.12 = bf16[256,256]{1,0:T(8,128)(2,1)S(1)} collective-permute-done((bf16[256,256]{1,0:T(8,128)(2,1)S(1)}, bf16[256,256]{1,0:T(8,128)(2,1)S(1)}, u32[]{:S(2)}, u32[]{:S(2)}) %collective-permute-start.12) | collective-permute-done | bytes 131104 | tf_op jit(solution)/shard_map/ppermute | solution.py:257
  26.6 1.5 collective-permute-start.11
  28.1 0.9 collective-permute-start.10
  29.0 1.3 collective-permute-start.9
  30.3 2.6 %collective-permute-start.8 = (bf16[256,256]{1,0:T(8,128)(2,1)S(1)}, bf16[256,256]{1,0:T(8,128)(2,1)S(1)}, u32[]{:S(2)}, u32[]{:S(2)}) collective-permute-start(bf16[256,256]{1,0:T(8,128)(2,1)S(1)} %get-tuple-element.16), channel_id=1, source_target_pairs={{2,0},{3,1},{0,2},{1,3},{6,4},{7,5},{4,6},{5,7},{10,8},{11,9},{8,1... | collective-permute-start | bytes 393224 | tf_op jit(solution)/shard_map/ppermute | solution.py:257
  32.9 1.1 collective-permute-start.7
  34.0 0.8 copy.13
  34.8 0.7 reshape.36.lists
  35.4 0.7 pad_add_fusion.ids
  36.1 5.9 %pack.1 = (bf16[16,4,128,128]{3,2,1,0:T(8,128)(2,1)}, bf16[8,128,128]{2,1,0:T(8,128)(2,1)}) custom-call(s32[2]{0:T(128)} %pad_add_fusion.ids, s32[1024]{0:T(1024)} %reshape.36.lists, s32[128]{0:T(128)} %orders.7, bf16[512,256]{1,0:T(8,128)(2,1)} %refs_0_.1, bf16[512,256]{1,0:T(8,128)(2,1)} %copy-done.16, bf16[512,256]{1,0:T(8,128)(2,1)} %copy-done.15, ...), custom_call_target="tpu_custom_call" | custom-call | tf_op jit(solution)/shard_map/pack/pallas_call | solution.py:278
  42.1 0.6 copy-done.21
  42.7 0.1 copy-done.24
  42.8 0.0 copy-done.26
  42.8 3.7 %all-to-all-start = ((bf16[16,4,128,128]{3,2,1,0:T(8,128)(2,1)}), bf16[16,4,128,128]{3,2,1,0:T(8,128)(2,1)S(1)}, u32[]{:S(2)}, u32[]{:S(2)}) async-start(bf16[16,4,128,128]{3,2,1,0:T(8,128)(2,1)} %get-tuple-element.14), calls=%async_computation | async-start | bytes 4194304 | tf_op jit(solution)/shard_map/all_to_all | solution.py:290
  47.2 0.7 reshape.37.pattern
  47.9 24.3 %all-to-all-done.tiles = bf16[16,4,128,128]{3,2,1,0:T(8,128)(2,1)S(1)} async-done(((bf16[16,4,128,128]{3,2,1,0:T(8,128)(2,1)}), bf16[16,4,128,128]{3,2,1,0:T(8,128)(2,1)S(1)}, u32[]{:S(2)}, u32[]{:S(2)}) %all-to-all-start) | async-done | bytes 2097184 | tf_op jit(solution)/shard_map/all_to_all | solution.py:290
  72.1 1.4 copy-done.1
  73.5 16.7 %solve.1 = bf16[8,32,128]{2,1,0:T(8,128)(2,1)} custom-call(s32[2]{0:T(128)} %pad_add_fusion.ids, s32[1024]{0:T(1024)} %reshape.36.lists, s32[128]{0:T(128)} %orders.7, s32[1024]{0:T(1024)} %reshape.37.pattern, f32[1]{0:T(128)S(6)} %copy.14.shift, bf16[16,4,128,128]{3,2,1,0:T(8,128)(2,1)} %copy-done.1, bf16[8,128,128]{2,1,0:T(8,128)(2,1)} %get-tuple-element.15.first), custom_call_target="tpu_custom_call" | custom-call | tf_op jit(solution)/shard_map/solve/pallas_call | solution.py:293
  90.2 19.5 %all-gather = bf16[64,32,128]{2,1,0:T(8,128)(2,1)} all-gather(bf16[8,32,128]{2,1,0:T(8,128)(2,1)} %solve.1), channel_id=2, replica_groups=mesh['z'=4,'core'=2,'c0'=4,'c1'=4] {'z','core'}, dimensions={0}, use_global_device_ids=true | all-gather | bytes 589824 | tf_op jit(solution)/shard_map/all_gather | solution.py:306
  109.7 4.0 %spread.1 = bf16[16,8,2,32,128]{4,3,2,1,0:T(8,128)(2,1)} custom-call(s32[2]{0:T(128)} %pad_add_fusion.ids, s32[1024]{0:T(1024)} %reshape.36.lists, s32[128]{0:T(128)} %orders.7, bf16[8,8,32,128]{3,2,1,0:T(8,128)(2,1)} %bitcast.11), custom_call_target="tpu_custom_call" | custom-call | tf_op jit(solution)/shard_map/spread/pallas_call | solution.py:307
  113.7 3.8 %all-to-all-start.1 = ((bf16[16,8,2,32,128]{4,3,2,1,0:T(8,128)(2,1)}), bf16[16,8,2,32,128]{4,3,2,1,0:T(8,128)(2,1)S(1)}, u32[]{:S(2)}, u32[]{:S(2)}) async-start(bf16[16,8,2,32,128]{4,3,2,1,0:T(8,128)(2,1)} %spread.1), calls=%async_computation.1 | async-start | bytes 4194304 | tf_op jit(solution)/shard_map/all_to_all | solution.py:315
  117.6 0.1 pad_maximum_fusion.1.b0
  117.7 1.3 collective-permute-start.18
  119.0 2.4 %collective-permute-start.17 = (bf16[4,256,256]{2,1,0:T(8,128)(2,1)S(1)}, bf16[4,256,256]{2,1,0:T(8,128)(2,1)S(1)}, u32[]{:S(2)}, u32[]{:S(2)}) collective-permute-start(bf16[4,256,256]{2,1,0:T(8,128)(2,1)S(1)} %pad_maximum_fusion.1.b0), channel_id=1, source_target_pairs={{2,0},{3,1},{0,2},{1,3},{6,4},{7,5},{4,6},{5,7},{10,8},{11,9},{8,1... | collective-permute-start | bytes 1572872 | tf_op jit(solution)/shard_map/ppermute | solution.py:257
  121.4 1.2 collective-permute-start.16
  122.5 1.0 pad_maximum_fusion.a0
  123.6 1.3 collective-permute-start.15
  124.9 2.4 %collective-permute-start.14 = (bf16[4,256,256]{2,1,0:T(8,128)(2,1)S(1)}, bf16[4,256,256]{2,1,0:T(8,128)(2,1)S(1)}, u32[]{:S(2)}, u32[]{:S(2)}) collective-permute-start(bf16[4,256,256]{2,1,0:T(8,128)(2,1)S(1)} %pad_maximum_fusion.a0), channel_id=1, source_target_pairs={{8,0},{12,4},{0,8},{4,12},{9,1},{13,5},{1,9},{5,13},{10,2},{14,6},... | collective-permute-start | bytes 1572872 | tf_op jit(solution)/shard_map/ppermute | solution.py:257
  127.3 27.5 %collective-permute-done.18.b3 = bf16[4,256,256]{2,1,0:T(8,128)(2,1)S(1)} collective-permute-done((bf16[4,256,256]{2,1,0:T(8,128)(2,1)S(1)}, bf16[4,256,256]{2,1,0:T(8,128)(2,1)S(1)}, u32[]{:S(2)}, u32[]{:S(2)}) %collective-permute-start.18) | collective-permute-done | bytes 524320 | tf_op jit(solution)/shard_map/ppermute | solution.py:257
  154.8 2.5 %collective-permute-start.13 = (bf16[4,256,256]{2,1,0:T(8,128)(2,1)S(1)}, bf16[4,256,256]{2,1,0:T(8,128)(2,1)}, u32[]{:S(2)}, u32[]{:S(2)}) collective-permute-start(bf16[4,256,256]{2,1,0:T(8,128)(2,1)S(1)} %pad_maximum_fusion.a0), channel_id=1, source_target_pairs={{4,0},{8,4},{12,8},{0,12},{5,1},{9,5},{13,9},{1,13},{6,2},{10,6},{... | collective-permute-start | bytes 1572872 | tf_op jit(solution)/shard_map/ppermute | solution.py:257
  157.3 8.6 %collective-permute-done.17.b2 = bf16[4,256,256]{2,1,0:T(8,128)(2,1)S(1)} collective-permute-done((bf16[4,256,256]{2,1,0:T(8,128)(2,1)S(1)}, bf16[4,256,256]{2,1,0:T(8,128)(2,1)S(1)}, u32[]{:S(2)}, u32[]{:S(2)}) %collective-permute-start.17) | collective-permute-done | bytes 524320 | tf_op jit(solution)/shard_map/ppermute | solution.py:257
  166.0 0.2 collective-permute-done.16.b1
  166.2 2.6 %collective-permute-done.14.a2 = bf16[4,256,256]{2,1,0:T(8,128)(2,1)S(1)} collective-permute-done((bf16[4,256,256]{2,1,0:T(8,128)(2,1)S(1)}, bf16[4,256,256]{2,1,0:T(8,128)(2,1)S(1)}, u32[]{:S(2)}, u32[]{:S(2)}) %collective-permute-start.14) | collective-permute-done | bytes 524320 | tf_op jit(solution)/shard_map/ppermute | solution.py:257
  168.8 0.8 copy-done.8
  169.6 7.6 %hp.1.refs_0_ = bf16[512,256]{1,0:T(8,128)(2,1)} custom-call(s32[2]{0:T(128)} %pad_add_fusion.ids, s32[1024]{0:T(1024)} %reshape.36.lists, s32[128]{0:T(128)} %orders.7, s32[1024]{0:T(1024)} %reshape.37.pattern, bf16[4,256,256]{2,1,0:T(8,128)(2,1)} %copy-done.3, bf16[4,256,256]{2,1,0:T(8,128)(2,1)} %collective-permute-done.13.a1, ...), custom_call_target="tpu_custom_call" | custom-call | tf_op jit(solution)/shard_map/hp/pallas_call | solution.py:316
  177.2 1.0 collective-permute-start.21
  178.3 2.4 %collective-permute-start.20 = (bf16[512,256]{1,0:T(8,128)(2,1)}, bf16[512,256]{1,0:T(8,128)(2,1)S(1)}, u32[]{:S(2)}, u32[]{:S(2)}) collective-permute-start(bf16[512,256]{1,0:T(8,128)(2,1)} %hp.1.refs_0_), channel_id=1, source_target_pairs={{64,0},{96,32},{0,64},{32,96},{65,1},{97,33},{1,65},{33,97},{66,2}... | collective-permute-start | bytes 786440 | tf_op jit(solution)/shard_map/ppermute | solution.py:257
  180.7 0.0 collective-permute-start.19
  180.8 1.7 collective-permute-start.22
  182.5 3.0 %collective-permute-done.21.refs_3_ = bf16[512,256]{1,0:T(8,128)(2,1)S(1)} collective-permute-done((bf16[512,256]{1,0:T(8,128)(2,1)}, bf16[512,256]{1,0:T(8,128)(2,1)S(1)}, u32[]{:S(2)}, u32[]{:S(2)}) %collective-permute-start.21) | collective-permute-done | bytes 262176 | tf_op jit(solution)/shard_map/ppermute | solution.py:257
  185.5 2.8 %collective-permute-start.25 = (bf16[512,256]{1,0:T(8,128)(2,1)S(1)}, bf16[512,256]{1,0:T(8,128)(2,1)S(1)}, u32[]{:S(2)}, u32[]{:S(2)}) collective-permute-start(bf16[512,256]{1,0:T(8,128)(2,1)S(1)} %collective-permute-done.21.refs_3_), channel_id=1, source_target_pairs={{0,16},{16,0},{1,17},{17,1},{2,18},{18,2},{3,19},{19,3},{4,20},{20... | collective-permute-start | bytes 786440 | tf_op jit(solution)/shard_map/ppermute | solution.py:261
  188.3 3.6 %collective-permute-done.20.refs_2_ = bf16[512,256]{1,0:T(8,128)(2,1)S(1)} collective-permute-done((bf16[512,256]{1,0:T(8,128)(2,1)}, bf16[512,256]{1,0:T(8,128)(2,1)S(1)}, u32[]{:S(2)}, u32[]{:S(2)}) %collective-permute-start.20) | collective-permute-done | bytes 262176 | tf_op jit(solution)/shard_map/ppermute | solution.py:257
  191.9 1.9 collective-permute-start.24
  193.8 0.1 collective-permute-start.23
  193.9 0.1 and_reduce_fusion
  194.0 0.1 copy.12
  194.1 0.7 reshape.38.present
  194.9 0.2 collective-permute-done.24.refs_6_
  195.1 0.4 collective-permute-done.23.refs_5_
  195.5 0.0 copy-done.12
  195.6 0.1 copy-done.13
  195.7 1.4 copy-done
  197.0 5.8 %final.1 = (bf16[512,256]{1,0:T(8,128)(2,1)}, f32[512,256]{1,0:T(8,128)}) custom-call(s32[2]{0:T(128)} %pad_add_fusion.ids, s32[512]{0:T(512)} %reshape.38.present, bf16[16,8,2,32,128]{4,3,2,1,0:T(8,128)(2,1)} %copy-done, bf16[512,256]{1,0:T(8,128)(2,1)} %hp.1.refs_0_, bf16[512,256]{1,0:T(8,128)(2,1)} %copy-done.11, bf16[512,256]{1,0:T(8,128)(2,1)} %copy-done.10, ...), custom_call_target="tpu_custom_call" | custom-call | tf_op jit(solution)/shard_map/final/pallas_call | solution.py:333
  (71 shorter events, 0.2 us)
Async XLA Ops:
  0.6 10.9 %collective-permute-start.2 = (bf16[512,256]{1,0:T(8,128)(2,1)}, bf16[512,256]{1,0:T(8,128)(2,1)S(1)}, u32[]{:S(2)}, u32[]{:S(2)}) collective-permute-start(bf16[512,256]{1,0:T(8,128)(2,1)} %refs_0_.1), channel_id=1, source_target_pairs={{96,0},{0,32},{32,64},{64,96},{97,1},{1,33},{33,65},{65,97},{98,2}... | collective-permute-start | bytes 786440 | tf_op jit(solution)/shard_map/ppermute | solution.py:257
  3.2 14.9 %collective-permute-start.1 = (bf16[512,256]{1,0:T(8,128)(2,1)}, bf16[512,256]{1,0:T(8,128)(2,1)S(1)}, u32[]{:S(2)}, u32[]{:S(2)}) collective-permute-start(bf16[512,256]{1,0:T(8,128)(2,1)} %refs_0_.1), channel_id=1, source_target_pairs={{64,0},{96,32},{0,64},{32,96},{65,1},{97,33},{1,65},{33,97},{66,2}... | collective-permute-start | bytes 786440 | tf_op jit(solution)/shard_map/ppermute | solution.py:257
  6.5 13.1 %collective-permute-start = (bf16[512,256]{1,0:T(8,128)(2,1)}, bf16[512,256]{1,0:T(8,128)(2,1)S(1)}, u32[]{:S(2)}, u32[]{:S(2)}) collective-permute-start(bf16[512,256]{1,0:T(8,128)(2,1)} %refs_0_.1), channel_id=1, source_target_pairs={{32,0},{64,32},{96,64},{0,96},{33,1},{65,33},{97,65},{1,97},{34,2}... | collective-permute-start | bytes 786440 | tf_op jit(solution)/shard_map/ppermute | solution.py:257
  7.2 20.9 %collective-permute-start.3 = (bf16[512,256]{1,0:T(8,128)(2,1)}, bf16[512,256]{1,0:T(8,128)(2,1)S(1)}, u32[]{:S(2)}, u32[]{:S(2)}) collective-permute-start(bf16[512,256]{1,0:T(8,128)(2,1)} %refs_0_.1), channel_id=1, source_target_pairs={{0,16},{16,0},{1,17},{17,1},{2,18},{18,2},{3,19},{19,3},{4,20},{20... | collective-permute-start | bytes 786440 | tf_op jit(solution)/shard_map/ppermute | solution.py:261
  11.5 24.6 %copy-start.14 = (bf16[512,256]{1,0:T(8,128)(2,1)}, bf16[512,256]{1,0:T(8,128)(2,1)S(1)}, u32[]{:S(2)}) copy-start(bf16[512,256]{1,0:T(8,128)(2,1)S(1)} %collective-permute-done.2.refs_3_) | copy-start | bytes 786436
  11.5 17.5 %collective-permute-start.6 = (bf16[512,256]{1,0:T(8,128)(2,1)S(1)}, bf16[512,256]{1,0:T(8,128)(2,1)S(1)}, u32[]{:S(2)}, u32[]{:S(2)}) collective-permute-start(bf16[512,256]{1,0:T(8,128)(2,1)S(1)} %collective-permute-done.2.refs_3_), channel_id=1, source_target_pairs={{0,16},{16,0},{1,17},{17,1},{2,18},{18,2},{3,19},{19,3},{4,20},{20... | collective-permute-start | bytes 786440 | tf_op jit(solution)/shard_map/ppermute | solution.py:261
  18.0 18.1 %copy-start.15 = (bf16[512,256]{1,0:T(8,128)(2,1)}, bf16[512,256]{1,0:T(8,128)(2,1)S(1)}, u32[]{:S(2)}) copy-start(bf16[512,256]{1,0:T(8,128)(2,1)S(1)} %collective-permute-done.1.refs_2_) | copy-start | bytes 786436
  18.0 12.3 %collective-permute-start.5 = (bf16[512,256]{1,0:T(8,128)(2,1)S(1)}, bf16[512,256]{1,0:T(8,128)(2,1)S(1)}, u32[]{:S(2)}, u32[]{:S(2)}) collective-permute-start(bf16[512,256]{1,0:T(8,128)(2,1)S(1)} %collective-permute-done.1.refs_2_), channel_id=1, source_target_pairs={{0,16},{16,0},{1,17},{17,1},{2,18},{18,2},{3,19},{19,3},{4,20},{20... | collective-permute-start | bytes 786440 | tf_op jit(solution)/shard_map/ppermute | solution.py:261
  19.5 16.6 %copy-start.16 = (bf16[512,256]{1,0:T(8,128)(2,1)}, bf16[512,256]{1,0:T(8,128)(2,1)S(1)}, u32[]{:S(2)}) copy-start(bf16[512,256]{1,0:T(8,128)(2,1)S(1)} %collective-permute-done.refs_1_) | copy-start | bytes 786436
  19.5 13.4 %collective-permute-start.4 = (bf16[512,256]{1,0:T(8,128)(2,1)S(1)}, bf16[512,256]{1,0:T(8,128)(2,1)S(1)}, u32[]{:S(2)}, u32[]{:S(2)}) collective-permute-start(bf16[512,256]{1,0:T(8,128)(2,1)S(1)} %collective-permute-done.refs_1_), channel_id=1, source_target_pairs={{0,16},{16,0},{1,17},{17,1},{2,18},{18,2},{3,19},{19,3},{4,20},{20... | collective-permute-start | bytes 786440 | tf_op jit(solution)/shard_map/ppermute | solution.py:261
  20.6 5.9 %collective-permute-start.12 = (bf16[256,256]{1,0:T(8,128)(2,1)S(1)}, bf16[256,256]{1,0:T(8,128)(2,1)S(1)}, u32[]{:S(2)}, u32[]{:S(2)}) collective-permute-start(bf16[256,256]{1,0:T(8,128)(2,1)S(1)} %get-tuple-element.20), channel_id=1, source_target_pairs={{12,0},{0,4},{4,8},{8,12},{13,1},{1,5},{5,9},{9,13},{14,2},{2,6},{... | collective-permute-start | bytes 393224 | tf_op jit(solution)/shard_map/ppermute | solution.py:257
  26.6 15.4 %collective-permute-start.11 = (bf16[256,256]{1,0:T(8,128)(2,1)S(1)}, bf16[256,256]{1,0:T(8,128)(2,1)S(1)}, u32[]{:S(2)}, u32[]{:S(2)}) collective-permute-start(bf16[256,256]{1,0:T(8,128)(2,1)S(1)} %get-tuple-element.20), channel_id=1, source_target_pairs={{8,0},{12,4},{0,8},{4,12},{9,1},{13,5},{1,9},{5,13},{10,2},{14,6},... | collective-permute-start | bytes 393224 | tf_op jit(solution)/shard_map/ppermute | solution.py:257
  28.1 8.0 %copy-start.17 = (bf16[512,256]{1,0:T(8,128)(2,1)}, bf16[512,256]{1,0:T(8,128)(2,1)S(1)}, u32[]{:S(2)}) copy-start(bf16[512,256]{1,0:T(8,128)(2,1)S(1)} %collective-permute-done.3.refs_4_) | copy-start | bytes 786436
  28.1 13.9 %collective-permute-start.10 = (bf16[256,256]{1,0:T(8,128)(2,1)S(1)}, bf16[256,256]{1,0:T(8,128)(2,1)S(1)}, u32[]{:S(2)}, u32[]{:S(2)}) collective-permute-start(bf16[256,256]{1,0:T(8,128)(2,1)S(1)} %get-tuple-element.20), channel_id=1, source_target_pairs={{4,0},{8,4},{12,8},{0,12},{5,1},{9,5},{13,9},{1,13},{6,2},{10,6},{... | collective-permute-start | bytes 393224 | tf_op jit(solution)/shard_map/ppermute | solution.py:257
  29.0 7.1 %copy-start.18 = (bf16[512,256]{1,0:T(8,128)(2,1)}, bf16[512,256]{1,0:T(8,128)(2,1)S(1)}, u32[]{:S(2)}) copy-start(bf16[512,256]{1,0:T(8,128)(2,1)S(1)} %collective-permute-done.6.refs_7_) | copy-start | bytes 786436
  29.0 13.1 %collective-permute-start.9 = (bf16[256,256]{1,0:T(8,128)(2,1)S(1)}, bf16[256,256]{1,0:T(8,128)(2,1)S(1)}, u32[]{:S(2)}, u32[]{:S(2)}) collective-permute-start(bf16[256,256]{1,0:T(8,128)(2,1)S(1)} %get-tuple-element.16), channel_id=1, source_target_pairs={{3,0},{0,1},{1,2},{2,3},{7,4},{4,5},{5,6},{6,7},{11,8},{8,9},{9,10... | collective-permute-start | bytes 393224 | tf_op jit(solution)/shard_map/ppermute | solution.py:257
  30.3 5.9 %copy-start.19 = (bf16[512,256]{1,0:T(8,128)(2,1)}, bf16[512,256]{1,0:T(8,128)(2,1)S(1)}, u32[]{:S(2)}) copy-start(bf16[512,256]{1,0:T(8,128)(2,1)S(1)} %collective-permute-done.5.refs_6_) | copy-start | bytes 786436
  30.3 11.8 %collective-permute-start.8 = (bf16[256,256]{1,0:T(8,128)(2,1)S(1)}, bf16[256,256]{1,0:T(8,128)(2,1)S(1)}, u32[]{:S(2)}, u32[]{:S(2)}) collective-permute-start(bf16[256,256]{1,0:T(8,128)(2,1)S(1)} %get-tuple-element.16), channel_id=1, source_target_pairs={{2,0},{3,1},{0,2},{1,3},{6,4},{7,5},{4,6},{5,7},{10,8},{11,9},{8,1... | collective-permute-start | bytes 393224 | tf_op jit(solution)/shard_map/ppermute | solution.py:257
  32.9 3.2 %copy-start.20 = (bf16[512,256]{1,0:T(8,128)(2,1)}, bf16[512,256]{1,0:T(8,128)(2,1)S(1)}, u32[]{:S(2)}) copy-start(bf16[512,256]{1,0:T(8,128)(2,1)S(1)} %collective-permute-done.4.refs_5_) | copy-start | bytes 786436
  32.9 9.2 %collective-permute-start.7 = (bf16[256,256]{1,0:T(8,128)(2,1)S(1)}, bf16[256,256]{1,0:T(8,128)(2,1)S(1)}, u32[]{:S(2)}, u32[]{:S(2)}) collective-permute-start(bf16[256,256]{1,0:T(8,128)(2,1)S(1)} %get-tuple-element.16), channel_id=1, source_target_pairs={{1,0},{2,1},{3,2},{0,3},{5,4},{6,5},{7,6},{4,7},{9,8},{10,9},{11,1... | collective-permute-start | bytes 393224 | tf_op jit(solution)/shard_map/ppermute | solution.py:257
  42.0 0.6 copy-start.21
  42.0 0.7 copy-start.24
  42.1 0.7 copy-start.23
  42.1 0.7 copy-start.26
  42.1 5.1 %copy-start.27 = (s32[32,32]{1,0:T(8,128)S(1)}, s32[32,32]{1,0:T(8,128)}, u32[]{:S(2)}) copy-start(s32[32,32]{1,0:T(8,128)} %param.6) | copy-start | bytes 12292
  42.8 29.3 %all-to-all-start = ((bf16[16,4,128,128]{3,2,1,0:T(8,128)(2,1)}), bf16[16,4,128,128]{3,2,1,0:T(8,128)(2,1)S(1)}, u32[]{:S(2)}, u32[]{:S(2)}) async-start(bf16[16,4,128,128]{3,2,1,0:T(8,128)(2,1)} %get-tuple-element.14), calls=%async_computation | async-start | bytes 4194304 | tf_op jit(solution)/shard_map/all_to_all | solution.py:290
  72.1 1.4 copy-start.1
  113.7 3.9 %copy-start.22 = (bf16[256,256]{1,0:T(8,128)(2,1)S(1)}, bf16[256,256]{1,0:T(8,128)(2,1)}, u32[]{:S(2)}) copy-start(bf16[256,256]{1,0:T(8,128)(2,1)} %copy-done.21) | copy-start | bytes 393220
  113.7 3.9 %copy-start.25 = (bf16[256,256]{1,0:T(8,128)(2,1)S(1)}, bf16[256,256]{1,0:T(8,128)(2,1)}, u32[]{:S(2)}) copy-start(bf16[256,256]{1,0:T(8,128)(2,1)} %copy-done.24) | copy-start | bytes 393220
  113.7 81.8 %all-to-all-start.1 = ((bf16[16,8,2,32,128]{4,3,2,1,0:T(8,128)(2,1)}), bf16[16,8,2,32,128]{4,3,2,1,0:T(8,128)(2,1)S(1)}, u32[]{:S(2)}, u32[]{:S(2)}) async-start(bf16[16,8,2,32,128]{4,3,2,1,0:T(8,128)(2,1)} %spread.1), calls=%async_computation.1 | async-start | bytes 4194304 | tf_op jit(solution)/shard_map/all_to_all | solution.py:315
  117.6 52.0 %copy-start.2 = (bf16[4,256,256]{2,1,0:T(8,128)(2,1)}, bf16[4,256,256]{2,1,0:T(8,128)(2,1)S(1)}, u32[]{:S(2)}) copy-start(bf16[4,256,256]{2,1,0:T(8,128)(2,1)S(1)} %pad_maximum_fusion.1.b0) | copy-start | bytes 1572868
  117.7 37.2 %collective-permute-start.18 = (bf16[4,256,256]{2,1,0:T(8,128)(2,1)S(1)}, bf16[4,256,256]{2,1,0:T(8,128)(2,1)S(1)}, u32[]{:S(2)}, u32[]{:S(2)}) collective-permute-start(bf16[4,256,256]{2,1,0:T(8,128)(2,1)S(1)} %pad_maximum_fusion.1.b0), channel_id=1, source_target_pairs={{3,0},{0,1},{1,2},{2,3},{7,4},{4,5},{5,6},{6,7},{11,8},{8,9},{9,10... | collective-permute-start | bytes 1572872 | tf_op jit(solution)/shard_map/ppermute | solution.py:257
  119.0 47.0 %collective-permute-start.17 = (bf16[4,256,256]{2,1,0:T(8,128)(2,1)S(1)}, bf16[4,256,256]{2,1,0:T(8,128)(2,1)S(1)}, u32[]{:S(2)}, u32[]{:S(2)}) collective-permute-start(bf16[4,256,256]{2,1,0:T(8,128)(2,1)S(1)} %pad_maximum_fusion.1.b0), channel_id=1, source_target_pairs={{2,0},{3,1},{0,2},{1,3},{6,4},{7,5},{4,6},{5,7},{10,8},{11,9},{8,1... | collective-permute-start | bytes 1572872 | tf_op jit(solution)/shard_map/ppermute | solution.py:257
  121.4 44.8 %collective-permute-start.16 = (bf16[4,256,256]{2,1,0:T(8,128)(2,1)S(1)}, bf16[4,256,256]{2,1,0:T(8,128)(2,1)S(1)}, u32[]{:S(2)}, u32[]{:S(2)}) collective-permute-start(bf16[4,256,256]{2,1,0:T(8,128)(2,1)S(1)} %pad_maximum_fusion.1.b0), channel_id=1, source_target_pairs={{1,0},{2,1},{3,2},{0,3},{5,4},{6,5},{7,6},{4,7},{9,8},{10,9},{11,1... | collective-permute-start | bytes 1572872 | tf_op jit(solution)/shard_map/ppermute | solution.py:257
  123.6 46.0 %copy-start.3 = (bf16[4,256,256]{2,1,0:T(8,128)(2,1)}, bf16[4,256,256]{2,1,0:T(8,128)(2,1)S(1)}, u32[]{:S(2)}) copy-start(bf16[4,256,256]{2,1,0:T(8,128)(2,1)S(1)} %pad_maximum_fusion.a0) | copy-start | bytes 1572868
  123.6 70.3 %copy-start.29 = (s32[128]{0:T(128)S(1)}, s32[128]{0:T(128)}, u32[]{:S(2)}) copy-start(s32[128]{0:T(128)} %orders.7) | copy-start | bytes 1540
  123.6 70.3 %copy-start.28 = (s32[128,8]{0,1:T(8,128)S(1)}, s32[128,8]{0,1:T(8,128)}, u32[]{:S(2)}) copy-start(s32[128,8]{0,1:T(8,128)} %param.7) | copy-start | bytes 12292
  123.6 42.6 %collective-permute-start.15 = (bf16[4,256,256]{2,1,0:T(8,128)(2,1)S(1)}, bf16[4,256,256]{2,1,0:T(8,128)(2,1)S(1)}, u32[]{:S(2)}, u32[]{:S(2)}) collective-permute-start(bf16[4,256,256]{2,1,0:T(8,128)(2,1)S(1)} %pad_maximum_fusion.a0), channel_id=1, source_target_pairs={{12,0},{0,4},{4,8},{8,12},{13,1},{1,5},{5,9},{9,13},{14,2},{2,6},{... | collective-permute-start | bytes 1572872 | tf_op jit(solution)/shard_map/ppermute | solution.py:257
  124.9 43.9 %collective-permute-start.14 = (bf16[4,256,256]{2,1,0:T(8,128)(2,1)S(1)}, bf16[4,256,256]{2,1,0:T(8,128)(2,1)S(1)}, u32[]{:S(2)}, u32[]{:S(2)}) collective-permute-start(bf16[4,256,256]{2,1,0:T(8,128)(2,1)S(1)} %pad_maximum_fusion.a0), channel_id=1, source_target_pairs={{8,0},{12,4},{0,8},{4,12},{9,1},{13,5},{1,9},{5,13},{10,2},{14,6},... | collective-permute-start | bytes 1572872 | tf_op jit(solution)/shard_map/ppermute | solution.py:257
  154.8 13.9 %copy-start.4 = (bf16[4,256,256]{2,1,0:T(8,128)(2,1)}, bf16[4,256,256]{2,1,0:T(8,128)(2,1)S(1)}, u32[]{:S(2)}) copy-start(bf16[4,256,256]{2,1,0:T(8,128)(2,1)S(1)} %collective-permute-done.18.b3) | copy-start | bytes 1572868
  154.8 14.8 %collective-permute-start.13 = (bf16[4,256,256]{2,1,0:T(8,128)(2,1)S(1)}, bf16[4,256,256]{2,1,0:T(8,128)(2,1)}, u32[]{:S(2)}, u32[]{:S(2)}) collective-permute-start(bf16[4,256,256]{2,1,0:T(8,128)(2,1)S(1)} %pad_maximum_fusion.a0), channel_id=1, source_target_pairs={{4,0},{8,4},{12,8},{0,12},{5,1},{9,5},{13,9},{1,13},{6,2},{10,6},{... | collective-permute-start | bytes 1572872 | tf_op jit(solution)/shard_map/ppermute | solution.py:257
  166.0 2.8 %copy-start.5 = (bf16[4,256,256]{2,1,0:T(8,128)(2,1)}, bf16[4,256,256]{2,1,0:T(8,128)(2,1)S(1)}, u32[]{:S(2)}) copy-start(bf16[4,256,256]{2,1,0:T(8,128)(2,1)S(1)} %collective-permute-done.17.b2) | copy-start | bytes 1572868
  166.2 2.6 %copy-start.6 = (bf16[4,256,256]{2,1,0:T(8,128)(2,1)}, bf16[4,256,256]{2,1,0:T(8,128)(2,1)S(1)}, u32[]{:S(2)}) copy-start(bf16[4,256,256]{2,1,0:T(8,128)(2,1)S(1)} %collective-permute-done.16.b1) | copy-start | bytes 1572868
  166.2 2.6 %copy-start.7 = (bf16[4,256,256]{2,1,0:T(8,128)(2,1)}, bf16[4,256,256]{2,1,0:T(8,128)(2,1)S(1)}, u32[]{:S(2)}) copy-start(bf16[4,256,256]{2,1,0:T(8,128)(2,1)S(1)} %collective-permute-done.15.a3) | copy-start | bytes 1572868
  168.8 0.8 copy-start.8
  177.2 8.3 %collective-permute-start.21 = (bf16[512,256]{1,0:T(8,128)(2,1)}, bf16[512,256]{1,0:T(8,128)(2,1)S(1)}, u32[]{:S(2)}, u32[]{:S(2)}) collective-permute-start(bf16[512,256]{1,0:T(8,128)(2,1)} %hp.1.refs_0_), channel_id=1, source_target_pairs={{96,0},{0,32},{32,64},{64,96},{97,1},{1,33},{33,65},{65,97},{98,2}... | collective-permute-start | bytes 786440 | tf_op jit(solution)/shard_map/ppermute | solution.py:257
  178.3 13.6 %collective-permute-start.20 = (bf16[512,256]{1,0:T(8,128)(2,1)}, bf16[512,256]{1,0:T(8,128)(2,1)S(1)}, u32[]{:S(2)}, u32[]{:S(2)}) collective-permute-start(bf16[512,256]{1,0:T(8,128)(2,1)} %hp.1.refs_0_), channel_id=1, source_target_pairs={{64,0},{96,32},{0,64},{32,96},{65,1},{97,33},{1,65},{33,97},{66,2}... | collective-permute-start | bytes 786440 | tf_op jit(solution)/shard_map/ppermute | solution.py:257
  180.7 13.1 %collective-permute-start.19 = (bf16[512,256]{1,0:T(8,128)(2,1)}, bf16[512,256]{1,0:T(8,128)(2,1)S(1)}, u32[]{:S(2)}, u32[]{:S(2)}) collective-permute-start(bf16[512,256]{1,0:T(8,128)(2,1)} %hp.1.refs_0_), channel_id=1, source_target_pairs={{32,0},{64,32},{96,64},{0,96},{33,1},{65,33},{97,65},{1,97},{34,2}... | collective-permute-start | bytes 786440 | tf_op jit(solution)/shard_map/ppermute | solution.py:257
  180.8 14.1 %collective-permute-start.22 = (bf16[512,256]{1,0:T(8,128)(2,1)}, bf16[512,256]{1,0:T(8,128)(2,1)S(1)}, u32[]{:S(2)}, u32[]{:S(2)}) collective-permute-start(bf16[512,256]{1,0:T(8,128)(2,1)} %hp.1.refs_0_), channel_id=1, source_target_pairs={{0,16},{16,0},{1,17},{17,1},{2,18},{18,2},{3,19},{19,3},{4,20},{20... | collective-permute-start | bytes 786440 | tf_op jit(solution)/shard_map/ppermute | solution.py:261
  185.5 10.0 %copy-start.9 = (bf16[512,256]{1,0:T(8,128)(2,1)}, bf16[512,256]{1,0:T(8,128)(2,1)S(1)}, u32[]{:S(2)}) copy-start(bf16[512,256]{1,0:T(8,128)(2,1)S(1)} %collective-permute-done.21.refs_3_) | copy-start | bytes 786436
  185.5 9.4 %collective-permute-start.25 = (bf16[512,256]{1,0:T(8,128)(2,1)S(1)}, bf16[512,256]{1,0:T(8,128)(2,1)S(1)}, u32[]{:S(2)}, u32[]{:S(2)}) collective-permute-start(bf16[512,256]{1,0:T(8,128)(2,1)S(1)} %collective-permute-done.21.refs_3_), channel_id=1, source_target_pairs={{0,16},{16,0},{1,17},{17,1},{2,18},{18,2},{3,19},{19,3},{4,20},{20... | collective-permute-start | bytes 786440 | tf_op jit(solution)/shard_map/ppermute | solution.py:261
  191.9 3.6 %copy-start.10 = (bf16[512,256]{1,0:T(8,128)(2,1)}, bf16[512,256]{1,0:T(8,128)(2,1)S(1)}, u32[]{:S(2)}) copy-start(bf16[512,256]{1,0:T(8,128)(2,1)S(1)} %collective-permute-done.20.refs_2_) | copy-start | bytes 786436
  191.9 3.2 %collective-permute-start.24 = (bf16[512,256]{1,0:T(8,128)(2,1)S(1)}, bf16[512,256]{1,0:T(8,128)(2,1)}, u32[]{:S(2)}, u32[]{:S(2)}) collective-permute-start(bf16[512,256]{1,0:T(8,128)(2,1)S(1)} %collective-permute-done.20.refs_2_), channel_id=1, source_target_pairs={{0,16},{16,0},{1,17},{17,1},{2,18},{18,2},{3,19},{19,3},{4,20},{20... | collective-permute-start | bytes 786440 | tf_op jit(solution)/shard_map/ppermute | solution.py:261
  193.8 1.7 copy-start.11
  193.8 1.7 collective-permute-start.23
  194.9 0.7 copy-start.12
  194.9 0.8 copy-start.13
  195.7 1.4 copy-start
where the time goes:
time: 204 us; the launch traced here: 203 us
  waiting for transfers between devices  83.1 us (41%)
  starting transfers between devices  48.4 us (24%)
  Pallas kernels  40 us (20%)
  blocking collectives  19.5 us (10%)
  local copies, waits for them, and re-layouts  8.36 us (4%)
    ppermute x18, waiting for transfers between devices, from_ring(): lax.ppermute(x, axis, [((i + k) % 4, i) for i in range(4)])  58.2 us
    ppermute x18, starting transfers between devices, from_ring(): lax.ppermute(x, axis, [((i + k) % 4, i) for i in range(4)])  29.9 us
    all_to_all x1, waiting for transfers between devices, steps(): tiles = lax.all_to_all(packed, COL, 0, 0, tiled=True)  24.3 us
    all_gather x1, blocking collectives, steps(): panels = lax.all_gather(panel, ROW, axis=0, tiled=False)  19.5 us
    pallas_call x1, Pallas kernels, steps(): pl.pallas_call(solve_kernel, out_shape=jax.ShapeDtypeStruct((MAXT, CW, TI...  16.7 us
    ppermute x8, starting transfers between devices, swapped(): return lax.ppermute(x, 'core', [(0, 1), (1, 0)])  10.9 us
    pallas_call x1, Pallas kernels, steps(): pl.pallas_call(hp_kernel, out_shape=jax.ShapeDtypeStruct((RT * TILE, WIDT...  7.63 us
    pallas_call x1, Pallas kernels, steps(): pl.pallas_call(pack_kernel, out_shape=(jax.ShapeDtypeStruct((COLS, 4, TIL...  5.86 us
  transfers between devices with their start and end apart: 28, of which 12 were waited for; matrix products, arithmetic and copies ran while one was open for 3% of the time, Pallas kernels for 7%

commit v1 on v0

v1 whole, which is shorter than its diff:
```python
import jax
import jax.numpy as jnp
from jax import lax
from jax.experimental import pallas as pl
from jax.experimental.pallas import tpu as pltpu
from jax.sharding import Mesh
from jax.sharding import PartitionSpec as P

TILE = 128
MAXT = 8
NB = 32
ROWS = 8
COLS = 16
CW = 32
N = MAXT * TILE
RT = NB // ROWS
CT = NB // COLS
WIDTH = CT * TILE
ROW = ("z", "core")
COL = ("c0", "c1")
F32 = jnp.float32
BF16 = jnp.bfloat16


def kept(pattern, a, b):
    return (pattern[a * NB + b] > 0) | (a == b)


def ring_owner(ids, k, part):
    return (ids[0] // 2 + k) % 4 * 2 + (ids[0] + part) % 2


def join_rows(ids, blocks, whole):
    for part in range(2):
        for k in range(4):
            start = pl.multiple_of(ring_owner(ids, k, part) * RT * TILE, RT * TILE)
            whole[pl.ds(start, RT * TILE), :] = blocks[part * 4 + k][...]


def cyclic(j, k):
    return 1 + (j - 1 + k) % (MAXT - 1)


def pack_kernel(ids, lists, orders, *refs):
    blocks, (out, first, strip, sems) = refs[:8], refs[8:]
    join_rows(ids, blocks, strip)

    def send(c, k, row, lanes):
        start = pl.multiple_of(row * TILE, TILE)
        lanes = pl.ds(pl.multiple_of(lanes * TILE, TILE), TILE)
        return pltpu.make_async_copy(
            strip.at[pl.ds(start, TILE), lanes], out.at[c, k], sems.at[c, k]
        )

    def one(c, _):
        s = c * ROWS + ids[0]
        which = jnp.int32(1)
        for j in range(2, MAXT):
            hit = (lists[s * MAXT + j] // CT == ids[1]) & (j < orders[s])
            which = jnp.where(hit, j, which)
        side = lists[s * MAXT + which] % CT
        for k in range(4):
            send(c, k, lists[s * MAXT + cyclic(which, k)], side).start()
        return 0

    lax.fori_loop(0, COLS, one, 0)

    def tile(a, lanes):
        return strip[pl.ds(pl.multiple_of(a * TILE, TILE), TILE), lanes]

    own = (ids[1] * ROWS + ids[0]) * MAXT
    lanes = pl.ds(pl.multiple_of(lists[own] % CT * TILE, TILE), TILE)
    for i in range(MAXT):
        first[i] = tile(lists[own + i], lanes)

    def done(c, _):
        for k in range(4):
            send(c, k, 0, 0).wait()
        return 0

    lax.fori_loop(0, COLS, done, 0)


def solve_kernel(ids, lists, orders, pattern, shift, tiles, first, panel, x, f, y, d):
    s = ids[1] * ROWS + ids[0]
    order = orders[s]
    potential = shift[0]
    names = [lists[s * MAXT + j] for j in range(MAXT)]
    rows = lax.broadcasted_iota(jnp.int32, (TILE, TILE), 0)
    cols = lax.broadcasted_iota(jnp.int32, (TILE, TILE), 1)
    eye = jnp.where(rows == cols, 1.0, 0.0).astype(F32)

    def put(i, j, tile):
        y[pl.ds(i * TILE, TILE), pl.ds(j * TILE, TILE)] = tile

    def masked(i, j, tile):
        both = kept(pattern, names[i], names[j]) & (i < order) & (j < order)
        return jnp.where(both, tile, jnp.zeros_like(tile))

    for i in range(MAXT):
        tile = masked(i, 0, first[i])
        put(i, 0, tile)
        if i:
            put(0, i, tile.T)
            for k in range(4):
                tile = masked(cyclic(i, k), i, tiles[names[i] // CT, k])
                put(cyclic(i, k), i, tile)
                if k:
                    put(i, cyclic(i, k), tile.T)

    def shifted(i, j):
        tile = y[pl.ds(i * TILE, TILE), pl.ds(j * TILE, TILE)].astype(F32)
        if i == j:
            tile = tile - jnp.where(i < order, potential, 0.0) * eye
        return tile

    largest = jnp.zeros((), F32)
    for i in range(MAXT):
        total = jnp.zeros((TILE, TILE), F32)
        for j in range(MAXT):
            tile = shifted(i, j)
            total = total + tile * tile
        largest = jnp.maximum(largest, jnp.max(jnp.sum(total, axis=1)))
    root = jnp.sqrt(jnp.full((8, TILE), largest + 1e-06, F32))
    inverse = (1.0 / (jnp.abs(potential) + 2.0 * root))[0:1, :]
    for i in range(MAXT):
        for j in range(MAXT):
            x[pl.ds(i * TILE, TILE), pl.ds(j * TILE, TILE)] = (shifted(i, j) * inverse).astype(BF16)

    band = 512
    brow = lax.broadcasted_iota(jnp.int32, (band, N), 0)
    bcol = lax.broadcasted_iota(jnp.int32, (band, N), 1)

    def step(source, target):
        def square(b, _):
            here = pl.ds(pl.multiple_of(b * band, band), band)
            q = jnp.dot(source[here, :], source[...], preferred_element_type=F32)
            diag = jnp.where(brow + b * band == bcol, 1.5, 0.0)
            f[here, :] = (diag - 0.5 * q).astype(BF16)
            return 0

        def apply(b, _):
            here = pl.ds(pl.multiple_of(b * band, band), band)
            target[here, :] = jnp.dot(
                source[here, :], f[...], preferred_element_type=F32
            ).astype(BF16)
            return 0

        lax.fori_loop(0, N // band, square, 0)
        lax.fori_loop(0, N // band, apply, 0)

    step(x, y)
    step(y, x)
    head = pl.ds(0, TILE)
    prow = lax.broadcasted_iota(jnp.int32, (N, TILE), 0)
    pcol = lax.broadcasted_iota(jnp.int32, (N, TILE), 1)
    q = jnp.dot(x[...], x[:, head], preferred_element_type=F32)
    f[:, head] = (jnp.where(prow == pcol, 1.5, 0.0) - 0.5 * q).astype(BF16)
    z = jnp.dot(x[...], f[:, head], preferred_element_type=F32)
    dens = jnp.where(prow == pcol, 0.5, 0.0) - 0.5 * z
    for i in range(MAXT):
        d[:, pl.ds(i * TILE, TILE)] = dens[i * TILE : (i + 1) * TILE, :].T
    offset = pl.multiple_of(s % (TILE // CW) * CW, CW)
    for i in range(MAXT):
        panel[i] = d[pl.ds(offset, CW), pl.ds(i * TILE, TILE)].astype(BF16)


def spread_kernel(ids, lists, orders, panels, out, mine, sems):
    mine[...] = jnp.zeros_like(mine)
    for k in range(ROWS):
        s = ids[1] * ROWS + k
        for i in range(MAXT):
            group = lists[s * MAXT + i] // CT

            @pl.when((i < orders[s]) & (group // (RT // CT) == ids[0]))
            def _():
                mine[k, group % (RT // CT)] = panels[k, i]

    copies = [pltpu.make_async_copy(mine, out.at[c], sems.at[c]) for c in range(COLS)]
    for copy in copies:
        copy.start()
    for copy in copies:
        copy.wait()


def hp_kernel(ids, lists, orders, pattern, a0, a1, a2, a3, b0, b1, b2, b3, panels, hp, pt, wide):
    c0 = ids[1] // 4
    c1 = ids[1] % 4
    for k in range(4):
        for m in range(4):
            first = (c0 + k) % 4 * 4 + (c1 + m) % 4
            second = (c0 + m) % 4 * 4 + (c1 + k) % 4
            for part, ref, col in ((0, (a0, a1, a2, a3)[k], first), (1, (b0, b1, b2, b3)[k], second)):
                for i in range(RT // 2):
                    for j in range(CT):
                        a = part * (RT // 2) + i
                        b = col * CT + j
                        tile = ref[m, pl.ds(i * TILE, TILE), pl.ds(j * TILE, TILE)]
                        live = kept(pattern, ids[0] * RT + a, b)
                        wide[
                            pl.ds(a * TILE, TILE), pl.ds(pl.multiple_of(b * TILE, TILE), TILE)
                        ] = jnp.where(live, tile, jnp.zeros_like(tile))
    pt[...] = jnp.zeros_like(pt)
    for k in range(ROWS):
        s = ids[1] * ROWS + k
        for i in range(MAXT):

            @pl.when(i < orders[s])
            def _():
                where = pl.multiple_of(lists[s * MAXT + i] * TILE, TILE)
                pt[pl.ds(k * CW, CW), pl.ds(where, TILE)] = panels[k, i]

    hp[...] = lax.dot_general(
        wide[...], pt[...], (((1,), (1,)), ((), ())), preferred_element_type=F32
    ).astype(BF16)


def final_kernel(ids, present, pieces, *refs):
    blocks = refs[:8]
    density, php, pt, hp = refs[8:]
    join_rows(ids, blocks, hp)

    def place(c, _):
        for r in range(ROWS):
            s = c * ROWS + r
            here = pl.ds(pl.multiple_of(s * CW, CW), CW)
            for g in range(RT // CT):
                piece = pieces[c, r, g]
                for a in range(g * CT, g * CT + CT):
                    live = present[s * RT + a] > 0
                    pt[here, pl.ds(a * TILE, TILE)] = jnp.where(live, piece, jnp.zeros_like(piece))
        return 0

    lax.fori_loop(0, COLS, place, 0)
    php[...] = lax.dot_general(
        pt[...], hp[...], (((0,), (0,)), ((), ())), preferred_element_type=F32
    )
    mine = pt[pl.ds(pl.multiple_of(ids[1] * WIDTH, WIDTH), WIDTH), :]
    density[...] = mine.T


def from_ring(x, axis):
    return [x] + [lax.ppermute(x, axis, [((i + k) % 4, i) for i in range(4)]) for k in range(1, 4)]


def swapped(x):
    return lax.ppermute(x, "core", [(0, 1), (1, 0)])


SMEM = pl.BlockSpec(memory_space=pltpu.SMEM)
LOCAL = pl.BlockSpec(memory_space=pltpu.VMEM)
FAR = pl.BlockSpec(memory_space=pl.ANY)


def call(kernel, outs, scratch, small, large, specs=LOCAL):
    return pl.pallas_call(
        kernel,
        out_shape=outs,
        in_specs=[SMEM] * len(small) + [LOCAL] * len(large),
        out_specs=specs,
        scratch_shapes=scratch,
        compiler_params=pltpu.CompilerParams(vmem_limit_bytes=24 << 20),
    )(*small, *[pltpu.with_memory_space_constraint(x, pltpu.VMEM) for x in large])


def call_solve(ids, lists, orders, pattern, shift, tiles, first):
    return call(
        solve_kernel,
        pltpu.VMEM((MAXT, CW, TILE), BF16),
        [pltpu.VMEM((N, N), BF16)] * 3 + [pltpu.VMEM((TILE, N), F32)],
        (ids, lists, orders, pattern, shift),
        (tiles, first),
    )


def steps(hamiltonian, pattern, tile_lists, orders, shift):
    row = lax.axis_index(ROW)
    col = lax.axis_index(COL)
    ids = jnp.stack([row, col]).astype(jnp.int32)
    lists = tile_lists.reshape(-1)
    flat_pattern = pattern.reshape(-1)
    half = RT * TILE // 2
    strip = from_ring(hamiltonian, "z")
    ahead = from_ring(hamiltonian[:half], "c1")
    across = from_ring(hamiltonian[half:], "c0")
    strip = strip + [swapped(x) for x in strip]
    packed, first = call(
        pack_kernel,
        (pltpu.HBM((COLS, 4, TILE, TILE), BF16), pltpu.VMEM((MAXT, TILE, TILE), BF16)),
        [pltpu.VMEM((NB * TILE, WIDTH), BF16), pltpu.SemaphoreType.DMA((COLS, 4))],
        (ids, lists, orders),
        strip,
        (FAR, LOCAL),
    )
    packed, ahead, across = lax.optimization_barrier((packed, ahead, across))
    tiles = lax.all_to_all(packed, COL, 0, 0, tiled=True)
    ahead = from_ring(jnp.stack(ahead), "c0")
    across = from_ring(jnp.stack(across), "c1")
    panel = call_solve(ids, lists, orders, flat_pattern, shift, tiles, first)
    panels = lax.all_gather(panel, ROW, axis=0, tiled=False)
    spread = call(
        spread_kernel,
        pltpu.HBM((COLS, ROWS, RT // CT, CW, TILE), BF16),
        [pltpu.VMEM((ROWS, RT // CT, CW, TILE), BF16), pltpu.SemaphoreType.DMA((COLS,))],
        (ids, lists, orders),
        (panels,),
        FAR,
    )
    arrived = lax.all_to_all(spread, COL, 0, 0, tiled=True)
    hp = call(
        hp_kernel,
        pltpu.VMEM((RT * TILE, WIDTH), BF16),
        [pltpu.VMEM((WIDTH, NB * TILE), BF16), pltpu.VMEM((RT * TILE, NB * TILE), BF16)],
        (ids, lists, orders, flat_pattern),
        (*ahead, *across, panels),
    )
    ours = from_ring(hp, "z")
    theirs = [swapped(x) for x in ours]
    own = row * RT + jnp.arange(RT, dtype=jnp.int32)
    live = jnp.arange(MAXT, dtype=jnp.int32)[None, :] < orders[:, None]
    present = jnp.any((tile_lists[:, None, :] == own[None, :, None]) & live[:, None, :], axis=2)
    density, php = call(
        final_kernel,
        (
            jax.ShapeDtypeStruct((RT * TILE, WIDTH), BF16),
            jax.ShapeDtypeStruct((RT * TILE, WIDTH), F32),
        ),
        [pltpu.VMEM((NB * TILE, RT * TILE), BF16), pltpu.VMEM((NB * TILE, WIDTH), BF16)],
        (ids, present.astype(jnp.int32).reshape(-1)),
        (arrived, *ours, *theirs),
        (LOCAL, LOCAL),
    )
    return density, php


def solution(mesh):
    fine = Mesh(mesh.devices.reshape(4, 2, 4, 4), ("z", "core", "c0", "c1"))
    split = P(ROW, COL)
    return jax.shard_map(
        steps,
        mesh=fine,
        in_specs=(split, P(), P(), P(), P()),
        out_specs=(split, split),
        check_vma=False,
    )
```

time: 204 us -> 190 us (0.931)
  Pallas kernels: 40 us -> 31.1 us
  local copies, waits for them, and re-layouts: 8.36 us -> 3.78 us
    pallas_call x5, Pallas kernels: 40 us -> 31.1 us  [call(): pl.pallas_call(kernel, out_shape=outs, in_specs=[SMEM] * len(small) + [LO...]
    unnamed x61 -> x11, local copies, waits for them, and re-layouts: 5.21 us -> 2.41 us
  transfers between devices with their start and end apart: 28 -> 28, of which waited for: 12 -> 12; matrix products, arithmetic and copies ran while one was open for 3% -> 2% of each run, Pallas kernels for 7% -> 4%
where the time goes in v1:
time: 190 us; the launch traced here: 188 us
  waiting for transfers between devices  83.5 us (44%)
  starting transfers between devices  48.1 us (25%)
  Pallas kernels  31.1 us (16%)
  blocking collectives  18.3 us (10%)
  local copies, waits for them, and re-layouts  3.78 us (2%)
  other arithmetic  2.13 us (1%)
    ppermute x18, waiting for transfers between devices, from_ring(): lax.ppermute(x, axis, [((i + k) % 4, i) for i in range(4)])  57.4 us
    pallas_call x5, Pallas kernels, call(): pl.pallas_call(kernel, out_shape=outs, in_specs=[SMEM] * len(small) + [LO...  31.1 us
    ppermute x18, starting transfers between devices, from_ring(): lax.ppermute(x, axis, [((i + k) % 4, i) for i in range(4)])  30 us
    all_to_all x1, waiting for transfers between devices, steps(): tiles = lax.all_to_all(packed, COL, 0, 0, tiled=True)  24.8 us
    all_gather x1, blocking collectives, steps(): panels = lax.all_gather(panel, ROW, axis=0, tiled=False)  18.3 us
    ppermute x8, starting transfers between devices, swapped(): return lax.ppermute(x, 'core', [(0, 1), (1, 0)])  10.7 us
  transfers between devices with their start and end apart: 28, of which 12 were waited for; matrix products, arithmetic and copies ran while one was open for 2% of the time, Pallas kernels for 4%

profile of v1, /device:TPU:1, one launch (start us, length us, event | category | flops | bytes accessed | tf_op | source)
XLA Modules:
  0.0 188.4 jit_solution(16604646446627248238)
XLA Ops:
  0.6 2.5 %collective-permute-start.2 = (bf16[512,256]{1,0:T(8,128)(2,1)}, bf16[512,256]{1,0:T(8,128)(2,1)S(1)}, u32[]{:S(2)}, u32[]{:S(2)}) collective-permute-start(bf16[512,256]{1,0:T(8,128)(2,1)} %refs_0_.1), channel_id=1, source_target_pairs={{96,0},{0,32},{32,64},{64,96},{97,1},{1,33},{33,65},{65,97},{98,2}... | collective-permute-start | bytes 786440 | tf_op jit(solution)/shard_map/ppermute | solution.py:243
  3.2 3.3 %collective-permute-start.1 = (bf16[512,256]{1,0:T(8,128)(2,1)}, bf16[512,256]{1,0:T(8,128)(2,1)S(1)}, u32[]{:S(2)}, u32[]{:S(2)}) collective-permute-start(bf16[512,256]{1,0:T(8,128)(2,1)} %refs_0_.1), channel_id=1, source_target_pairs={{64,0},{96,32},{0,64},{32,96},{65,1},{97,33},{1,65},{33,97},{66,2}... | collective-permute-start | bytes 786440 | tf_op jit(solution)/shard_map/ppermute | solution.py:243
  6.5 0.7 collective-permute-start
  7.2 1.5 collective-permute-start.3
  8.7 2.8 %collective-permute-done.2.refs_3_ = bf16[512,256]{1,0:T(8,128)(2,1)S(1)} collective-permute-done((bf16[512,256]{1,0:T(8,128)(2,1)}, bf16[512,256]{1,0:T(8,128)(2,1)S(1)}, u32[]{:S(2)}, u32[]{:S(2)}) %collective-permute-start.2) | collective-permute-done | bytes 262176 | tf_op jit(solution)/shard_map/ppermute | solution.py:243
  11.5 1.3 collective-permute-start.6
  12.7 5.3 %collective-permute-done.1.refs_2_ = bf16[512,256]{1,0:T(8,128)(2,1)S(1)} collective-permute-done((bf16[512,256]{1,0:T(8,128)(2,1)}, bf16[512,256]{1,0:T(8,128)(2,1)S(1)}, u32[]{:S(2)}, u32[]{:S(2)}) %collective-permute-start.1) | collective-permute-done | bytes 262176 | tf_op jit(solution)/shard_map/ppermute | solution.py:243
  18.0 1.5 collective-permute-start.5
  19.5 0.0 collective-permute-done.refs_1_
  19.5 0.0 collective-permute-start.4
  19.5 1.0 fusion
  20.5 1.3 collective-permute-start.12
  21.8 4.5 %collective-permute-done.12 = bf16[256,256]{1,0:T(8,128)(2,1)S(1)} collective-permute-done((bf16[256,256]{1,0:T(8,128)(2,1)S(1)}, bf16[256,256]{1,0:T(8,128)(2,1)S(1)}, u32[]{:S(2)}, u32[]{:S(2)}) %collective-permute-start.12) | collective-permute-done | bytes 131104 | tf_op jit(solution)/shard_map/ppermute | solution.py:243
  26.4 1.5 collective-permute-start.11
  27.9 0.9 collective-permute-start.10
  28.8 0.0 collective-permute-done.6.refs_7_
  28.8 1.3 collective-permute-start.9
  30.1 2.6 %collective-permute-start.8 = (bf16[256,256]{1,0:T(8,128)(2,1)S(1)}, bf16[256,256]{1,0:T(8,128)(2,1)S(1)}, u32[]{:S(2)}, u32[]{:S(2)}) collective-permute-start(bf16[256,256]{1,0:T(8,128)(2,1)S(1)} %get-tuple-element.16), channel_id=1, source_target_pairs={{2,0},{3,1},{0,2},{1,3},{6,4},{7,5},{4,6},{5,7},{10,8},{11,9},{8,1... | collective-permute-start | bytes 393224 | tf_op jit(solution)/shard_map/ppermute | solution.py:243
  32.7 0.0 collective-permute-done.4.refs_5_
  32.7 1.1 collective-permute-start.7
  33.8 0.8 copy.13
  34.5 0.1 reshape.36.lists
  34.7 0.1 pad_add_fusion.ids
  34.7 0.9 copy-done
  35.7 0.7 copy-done.1
  36.3 3.2 %shard_map.68 = (bf16[16,4,128,128]{3,2,1,0:T(8,128)(2,1)}, bf16[8,128,128]{2,1,0:T(8,128)(2,1)S(1)}) custom-call(s32[2]{0:T(128)S(1)} %pad_add_fusion.ids, s32[1024]{0:T(1024)S(1)} %reshape.36.lists, s32[128]{0:T(128)S(1)} %copy-done.1, bf16[512,256]{1,0:T(8,128)(2,1)S(1)} %copy-done, bf16[512,256]{1,0:T(8,128)(2,1)S(1)} %collective-permute-done.refs_1_, ...), custom_call_target="tpu_custom_call" | custom-call | tf_op jit(solution)/shard_map/pallas_call | solution.py:256
  39.6 0.0 copy-start.3
  39.6 0.0 copy-start.2
  39.6 3.7 %all-to-all-start = ((bf16[16,4,128,128]{3,2,1,0:T(8,128)(2,1)}), bf16[16,4,128,128]{3,2,1,0:T(8,128)(2,1)S(1)}, u32[]{:S(2)}, u32[]{:S(2)}) async-start(bf16[16,4,128,128]{3,2,1,0:T(8,128)(2,1)} %get-tuple-element.14), calls=%async_computation | async-start | bytes 4194304 | tf_op jit(solution)/shard_map/all_to_all | solution.py:296
  44.0 0.1 reshape.37.pattern
  44.0 24.8 %all-to-all-done.tiles = bf16[16,4,128,128]{3,2,1,0:T(8,128)(2,1)S(1)} async-done(((bf16[16,4,128,128]{3,2,1,0:T(8,128)(2,1)}), bf16[16,4,128,128]{3,2,1,0:T(8,128)(2,1)S(1)}, u32[]{:S(2)}, u32[]{:S(2)}) %all-to-all-start) | async-done | bytes 2097184 | tf_op jit(solution)/shard_map/all_to_all | solution.py:296
  68.8 15.1 %shard_map.69 = bf16[8,32,128]{2,1,0:T(8,128)(2,1)S(1)} custom-call(s32[2]{0:T(128)S(1)} %pad_add_fusion.ids, s32[1024]{0:T(1024)S(1)} %reshape.36.lists, s32[128]{0:T(128)S(1)} %copy-done.2, s32[1024]{0:T(1024)S(1)} %reshape.37.pattern, f32[1]{0:T(128)S(6)} %copy.14.shift, bf16[16,4,128,128]{3,2,1,0:T(8,128)(2,1)S(1)} %all-to-all-done.tiles, ...), custom_call_target="tpu_custom_call" | custom-call | tf_op jit(solution)/shard_map/pallas_call | solution.py:256
  84.0 18.3 %all-gather = bf16[64,32,128]{2,1,0:T(8,128)(2,1)S(1)} all-gather(bf16[8,32,128]{2,1,0:T(8,128)(2,1)S(1)} %shard_map.69), channel_id=2, replica_groups=mesh['z'=4,'core'=2,'c0'=4,'c1'=4] {'z','core'}, dimensions={0}, use_global_device_ids=true | all-gather | bytes 589824 | tf_op jit(solution)/shard_map/all_gather | solution.py:300
  102.3 3.5 %shard_map.70 = bf16[16,8,2,32,128]{4,3,2,1,0:T(8,128)(2,1)} custom-call(s32[2]{0:T(128)S(1)} %pad_add_fusion.ids, s32[1024]{0:T(1024)S(1)} %reshape.36.lists, s32[128]{0:T(128)S(1)} %copy-done.2, bf16[8,8,32,128]{3,2,1,0:T(8,128)(2,1)S(1)} %bitcast.11), custom_call_target="tpu_custom_call" | custom-call | tf_op jit(solution)/shard_map/pallas_call | solution.py:256
  105.8 3.7 %all-to-all-start.1 = ((bf16[16,8,2,32,128]{4,3,2,1,0:T(8,128)(2,1)}), bf16[16,8,2,32,128]{4,3,2,1,0:T(8,128)(2,1)S(1)}, u32[]{:S(2)}, u32[]{:S(2)}) async-start(bf16[16,8,2,32,128]{4,3,2,1,0:T(8,128)(2,1)} %shard_map.70), calls=%async_computation.1 | async-start | bytes 4194304 | tf_op jit(solution)/shard_map/all_to_all | solution.py:309
  109.5 1.0 pad_maximum_fusion.1.b0
  110.5 1.3 collective-permute-start.18
  111.8 2.4 %collective-permute-start.17 = (bf16[4,256,256]{2,1,0:T(8,128)(2,1)S(1)}, bf16[4,256,256]{2,1,0:T(8,128)(2,1)S(1)}, u32[]{:S(2)}, u32[]{:S(2)}) collective-permute-start(bf16[4,256,256]{2,1,0:T(8,128)(2,1)S(1)} %pad_maximum_fusion.1.b0), channel_id=1, source_target_pairs={{2,0},{3,1},{0,2},{1,3},{6,4},{7,5},{4,6},{5,7},{10,8},{11,9},{8,1... | collective-permute-start | bytes 1572872 | tf_op jit(solution)/shard_map/ppermute | solution.py:243
  114.2 1.2 collective-permute-start.16
  115.4 1.0 pad_maximum_fusion.a0
  116.4 0.0 copy-start.4
  116.4 1.3 collective-permute-start.15
  117.7 2.4 %collective-permute-start.14 = (bf16[4,256,256]{2,1,0:T(8,128)(2,1)S(1)}, bf16[4,256,256]{2,1,0:T(8,128)(2,1)S(1)}, u32[]{:S(2)}, u32[]{:S(2)}) collective-permute-start(bf16[4,256,256]{2,1,0:T(8,128)(2,1)S(1)} %pad_maximum_fusion.a0), channel_id=1, source_target_pairs={{8,0},{12,4},{0,8},{4,12},{9,1},{13,5},{1,9},{5,13},{10,2},{14,6},... | collective-permute-start | bytes 1572872 | tf_op jit(solution)/shard_map/ppermute | solution.py:243
  120.1 26.7 %collective-permute-done.18.b3 = bf16[4,256,256]{2,1,0:T(8,128)(2,1)S(1)} collective-permute-done((bf16[4,256,256]{2,1,0:T(8,128)(2,1)S(1)}, bf16[4,256,256]{2,1,0:T(8,128)(2,1)S(1)}, u32[]{:S(2)}, u32[]{:S(2)}) %collective-permute-start.18) | collective-permute-done | bytes 524320 | tf_op jit(solution)/shard_map/ppermute | solution.py:243
  146.8 2.5 %collective-permute-start.13 = (bf16[4,256,256]{2,1,0:T(8,128)(2,1)S(1)}, bf16[4,256,256]{2,1,0:T(8,128)(2,1)S(1)}, u32[]{:S(2)}, u32[]{:S(2)}) collective-permute-start(bf16[4,256,256]{2,1,0:T(8,128)(2,1)S(1)} %pad_maximum_fusion.a0), channel_id=1, source_target_pairs={{4,0},{8,4},{12,8},{0,12},{5,1},{9,5},{13,9},{1,13},{6,2},{10,6},{... | collective-permute-start | bytes 1572872 | tf_op jit(solution)/shard_map/ppermute | solution.py:243
  149.3 8.7 %collective-permute-done.17.b2 = bf16[4,256,256]{2,1,0:T(8,128)(2,1)S(1)} collective-permute-done((bf16[4,256,256]{2,1,0:T(8,128)(2,1)S(1)}, bf16[4,256,256]{2,1,0:T(8,128)(2,1)S(1)}, u32[]{:S(2)}, u32[]{:S(2)}) %collective-permute-start.17) | collective-permute-done | bytes 524320 | tf_op jit(solution)/shard_map/ppermute | solution.py:243
  158.0 0.1 collective-permute-done.16.b1
  158.1 2.9 %collective-permute-done.14.a2 = bf16[4,256,256]{2,1,0:T(8,128)(2,1)S(1)} collective-permute-done((bf16[4,256,256]{2,1,0:T(8,128)(2,1)S(1)}, bf16[4,256,256]{2,1,0:T(8,128)(2,1)S(1)}, u32[]{:S(2)}, u32[]{:S(2)}) %collective-permute-start.14) | collective-permute-done | bytes 524320 | tf_op jit(solution)/shard_map/ppermute | solution.py:243
  161.0 4.6 %shard_map.71.refs_0_ = bf16[512,256]{1,0:T(8,128)(2,1)S(1)} custom-call(s32[2]{0:T(128)S(1)} %pad_add_fusion.ids, s32[1024]{0:T(1024)S(1)} %reshape.36.lists, s32[128]{0:T(128)S(1)} %copy-done.2, s32[1024]{0:T(1024)S(1)} %reshape.37.pattern, bf16[4,256,256]{2,1,0:T(8,128)(2,1)S(1)} %pad_maximum_fusion.a0, ...), custom_call_target="tpu_custom_call" | custom-call | tf_op jit(solution)/shard_map/pallas_call | solution.py:256
  165.6 1.1 collective-permute-start.21
  166.7 2.4 %collective-permute-start.20 = (bf16[512,256]{1,0:T(8,128)(2,1)S(1)}, bf16[512,256]{1,0:T(8,128)(2,1)S(1)}, u32[]{:S(2)}, u32[]{:S(2)}) collective-permute-start(bf16[512,256]{1,0:T(8,128)(2,1)S(1)} %shard_map.71.refs_0_), channel_id=1, source_target_pairs={{64,0},{96,32},{0,64},{32,96},{65,1},{97,33},{1,65},{33,97},{66,2}... | collective-permute-start | bytes 786440 | tf_op jit(solution)/shard_map/ppermute | solution.py:243
  169.1 0.1 collective-permute-start.19
  169.2 1.7 collective-permute-start.22
  170.9 2.8 %collective-permute-done.21.refs_3_ = bf16[512,256]{1,0:T(8,128)(2,1)S(1)} collective-permute-done((bf16[512,256]{1,0:T(8,128)(2,1)S(1)}, bf16[512,256]{1,0:T(8,128)(2,1)S(1)}, u32[]{:S(2)}, u32[]{:S(2)}) %collective-permute-start.21) | collective-permute-done | bytes 262176 | tf_op jit(solution)/shard_map/ppermute | solution.py:243
  173.7 2.7 %collective-permute-start.25 = (bf16[512,256]{1,0:T(8,128)(2,1)S(1)}, bf16[512,256]{1,0:T(8,128)(2,1)}, u32[]{:S(2)}, u32[]{:S(2)}) collective-permute-start(bf16[512,256]{1,0:T(8,128)(2,1)S(1)} %collective-permute-done.21.refs_3_), channel_id=1, source_target_pairs={{0,16},{16,0},{1,17},{17,1},{2,18},{18,2},{3,19},{19,3},{4,20},{20... | collective-permute-start | bytes 786440 | tf_op jit(solution)/shard_map/ppermute | solution.py:247
  176.4 3.6 %collective-permute-done.20.refs_2_ = bf16[512,256]{1,0:T(8,128)(2,1)S(1)} collective-permute-done((bf16[512,256]{1,0:T(8,128)(2,1)S(1)}, bf16[512,256]{1,0:T(8,128)(2,1)S(1)}, u32[]{:S(2)}, u32[]{:S(2)}) %collective-permute-start.20) | collective-permute-done | bytes 262176 | tf_op jit(solution)/shard_map/ppermute | solution.py:243
  180.0 2.0 %collective-permute-start.24 = (bf16[512,256]{1,0:T(8,128)(2,1)S(1)}, bf16[512,256]{1,0:T(8,128)(2,1)}, u32[]{:S(2)}, u32[]{:S(2)}) collective-permute-start(bf16[512,256]{1,0:T(8,128)(2,1)S(1)} %collective-permute-done.20.refs_2_), channel_id=1, source_target_pairs={{0,16},{16,0},{1,17},{17,1},{2,18},{18,2},{3,19},{19,3},{4,20},{20... | collective-permute-start | bytes 786440 | tf_op jit(solution)/shard_map/ppermute | solution.py:247
  182.0 0.0 collective-permute-start.23
  182.0 0.1 and_reduce_fusion
  182.1 0.1 copy.12
  182.3 0.1 reshape.38.present
  182.4 0.9 collective-permute-done.24.refs_6_
  183.3 0.4 collective-permute-done.23.refs_5_
  183.7 4.8 %shard_map.72 = (bf16[512,256]{1,0:T(8,128)(2,1)}, f32[512,256]{1,0:T(8,128)}) custom-call(s32[2]{0:T(128)S(1)} %pad_add_fusion.ids, s32[512]{0:T(512)S(1)} %reshape.38.present, bf16[16,8,2,32,128]{4,3,2,1,0:T(8,128)(2,1)S(1)} %all-to-all-done.1.pieces, bf16[512,256]{1,0:T(8,128)(2,1)S(1)} %shard_map.71.refs_0_, ...), custom_call_target="tpu_custom_call" | custom-call | tf_op jit(solution)/shard_map/pallas_call | solution.py:256
  (21 shorter events, 0.1 us)
Async XLA Ops:
  0.6 10.9 %collective-permute-start.2 = (bf16[512,256]{1,0:T(8,128)(2,1)}, bf16[512,256]{1,0:T(8,128)(2,1)S(1)}, u32[]{:S(2)}, u32[]{:S(2)}) collective-permute-start(bf16[512,256]{1,0:T(8,128)(2,1)} %refs_0_.1), channel_id=1, source_target_pairs={{96,0},{0,32},{32,64},{64,96},{97,1},{1,33},{33,65},{65,97},{98,2}... | collective-permute-start | bytes 786440 | tf_op jit(solution)/shard_map/ppermute | solution.py:243
  3.2 14.9 %collective-permute-start.1 = (bf16[512,256]{1,0:T(8,128)(2,1)}, bf16[512,256]{1,0:T(8,128)(2,1)S(1)}, u32[]{:S(2)}, u32[]{:S(2)}) collective-permute-start(bf16[512,256]{1,0:T(8,128)(2,1)} %refs_0_.1), channel_id=1, source_target_pairs={{64,0},{96,32},{0,64},{32,96},{65,1},{97,33},{1,65},{33,97},{66,2}... | collective-permute-start | bytes 786440 | tf_op jit(solution)/shard_map/ppermute | solution.py:243
  6.5 13.1 %collective-permute-start = (bf16[512,256]{1,0:T(8,128)(2,1)}, bf16[512,256]{1,0:T(8,128)(2,1)S(1)}, u32[]{:S(2)}, u32[]{:S(2)}) collective-permute-start(bf16[512,256]{1,0:T(8,128)(2,1)} %refs_0_.1), channel_id=1, source_target_pairs={{32,0},{64,32},{96,64},{0,96},{33,1},{65,33},{97,65},{1,97},{34,2}... | collective-permute-start | bytes 786440 | tf_op jit(solution)/shard_map/ppermute | solution.py:243
  7.2 20.7 %collective-permute-start.3 = (bf16[512,256]{1,0:T(8,128)(2,1)}, bf16[512,256]{1,0:T(8,128)(2,1)S(1)}, u32[]{:S(2)}, u32[]{:S(2)}) collective-permute-start(bf16[512,256]{1,0:T(8,128)(2,1)} %refs_0_.1), channel_id=1, source_target_pairs={{0,16},{16,0},{1,17},{17,1},{2,18},{18,2},{3,19},{19,3},{4,20},{20... | collective-permute-start | bytes 786440 | tf_op jit(solution)/shard_map/ppermute | solution.py:247
  11.5 17.3 %collective-permute-start.6 = (bf16[512,256]{1,0:T(8,128)(2,1)S(1)}, bf16[512,256]{1,0:T(8,128)(2,1)S(1)}, u32[]{:S(2)}, u32[]{:S(2)}) collective-permute-start(bf16[512,256]{1,0:T(8,128)(2,1)S(1)} %collective-permute-done.2.refs_3_), channel_id=1, source_target_pairs={{0,16},{16,0},{1,17},{17,1},{2,18},{18,2},{3,19},{19,3},{4,20},{20... | collective-permute-start | bytes 786440 | tf_op jit(solution)/shard_map/ppermute | solution.py:247
  18.0 12.1 %collective-permute-start.5 = (bf16[512,256]{1,0:T(8,128)(2,1)S(1)}, bf16[512,256]{1,0:T(8,128)(2,1)S(1)}, u32[]{:S(2)}, u32[]{:S(2)}) collective-permute-start(bf16[512,256]{1,0:T(8,128)(2,1)S(1)} %collective-permute-done.1.refs_2_), channel_id=1, source_target_pairs={{0,16},{16,0},{1,17},{17,1},{2,18},{18,2},{3,19},{19,3},{4,20},{20... | collective-permute-start | bytes 786440 | tf_op jit(solution)/shard_map/ppermute | solution.py:247
  19.5 13.1 %collective-permute-start.4 = (bf16[512,256]{1,0:T(8,128)(2,1)S(1)}, bf16[512,256]{1,0:T(8,128)(2,1)S(1)}, u32[]{:S(2)}, u32[]{:S(2)}) collective-permute-start(bf16[512,256]{1,0:T(8,128)(2,1)S(1)} %collective-permute-done.refs_1_), channel_id=1, source_target_pairs={{0,16},{16,0},{1,17},{17,1},{2,18},{18,2},{3,19},{19,3},{4,20},{20... | collective-permute-start | bytes 786440 | tf_op jit(solution)/shard_map/ppermute | solution.py:247
  20.5 5.8 %collective-permute-start.12 = (bf16[256,256]{1,0:T(8,128)(2,1)S(1)}, bf16[256,256]{1,0:T(8,128)(2,1)S(1)}, u32[]{:S(2)}, u32[]{:S(2)}) collective-permute-start(bf16[256,256]{1,0:T(8,128)(2,1)S(1)} %get-tuple-element.20), channel_id=1, source_target_pairs={{12,0},{0,4},{4,8},{8,12},{13,1},{1,5},{5,9},{9,13},{14,2},{2,6},{... | collective-permute-start | bytes 393224 | tf_op jit(solution)/shard_map/ppermute | solution.py:243
  26.4 13.1 %collective-permute-start.11 = (bf16[256,256]{1,0:T(8,128)(2,1)S(1)}, bf16[256,256]{1,0:T(8,128)(2,1)S(1)}, u32[]{:S(2)}, u32[]{:S(2)}) collective-permute-start(bf16[256,256]{1,0:T(8,128)(2,1)S(1)} %get-tuple-element.20), channel_id=1, source_target_pairs={{8,0},{12,4},{0,8},{4,12},{9,1},{13,5},{1,9},{5,13},{10,2},{14,6},... | collective-permute-start | bytes 393224 | tf_op jit(solution)/shard_map/ppermute | solution.py:243
  27.9 11.6 %collective-permute-start.10 = (bf16[256,256]{1,0:T(8,128)(2,1)S(1)}, bf16[256,256]{1,0:T(8,128)(2,1)}, u32[]{:S(2)}, u32[]{:S(2)}) collective-permute-start(bf16[256,256]{1,0:T(8,128)(2,1)S(1)} %get-tuple-element.20), channel_id=1, source_target_pairs={{4,0},{8,4},{12,8},{0,12},{5,1},{9,5},{13,9},{1,13},{6,2},{10,6},{... | collective-permute-start | bytes 393224 | tf_op jit(solution)/shard_map/ppermute | solution.py:243
  28.8 10.8 %collective-permute-start.9 = (bf16[256,256]{1,0:T(8,128)(2,1)S(1)}, bf16[256,256]{1,0:T(8,128)(2,1)S(1)}, u32[]{:S(2)}, u32[]{:S(2)}) collective-permute-start(bf16[256,256]{1,0:T(8,128)(2,1)S(1)} %get-tuple-element.16), channel_id=1, source_target_pairs={{3,0},{0,1},{1,2},{2,3},{7,4},{4,5},{5,6},{6,7},{11,8},{8,9},{9,10... | collective-permute-start | bytes 393224 | tf_op jit(solution)/shard_map/ppermute | solution.py:243
  30.1 9.5 %collective-permute-start.8 = (bf16[256,256]{1,0:T(8,128)(2,1)S(1)}, bf16[256,256]{1,0:T(8,128)(2,1)S(1)}, u32[]{:S(2)}, u32[]{:S(2)}) collective-permute-start(bf16[256,256]{1,0:T(8,128)(2,1)S(1)} %get-tuple-element.16), channel_id=1, source_target_pairs={{2,0},{3,1},{0,2},{1,3},{6,4},{7,5},{4,6},{5,7},{10,8},{11,9},{8,1... | collective-permute-start | bytes 393224 | tf_op jit(solution)/shard_map/ppermute | solution.py:243
  32.7 6.9 %collective-permute-start.7 = (bf16[256,256]{1,0:T(8,128)(2,1)S(1)}, bf16[256,256]{1,0:T(8,128)(2,1)}, u32[]{:S(2)}, u32[]{:S(2)}) collective-permute-start(bf16[256,256]{1,0:T(8,128)(2,1)S(1)} %get-tuple-element.16), channel_id=1, source_target_pairs={{1,0},{2,1},{3,2},{0,3},{5,4},{6,5},{7,6},{4,7},{9,8},{10,9},{11,1... | collective-permute-start | bytes 393224 | tf_op jit(solution)/shard_map/ppermute | solution.py:243
  34.7 1.0 copy-start
  35.7 0.7 copy-start.1
  39.6 4.4 %copy-start.3 = (s32[32,32]{1,0:T(8,128)S(1)}, s32[32,32]{1,0:T(8,128)}, u32[]{:S(2)}) copy-start(s32[32,32]{1,0:T(8,128)} %param.6) | copy-start | bytes 12292
  39.6 29.3 %copy-start.2 = (s32[128]{0:T(128)S(1)}, s32[128]{0:T(128)}, u32[]{:S(2)}) copy-start(s32[128]{0:T(128)} %orders.7) | copy-start | bytes 1540
  39.6 29.3 %all-to-all-start = ((bf16[16,4,128,128]{3,2,1,0:T(8,128)(2,1)}), bf16[16,4,128,128]{3,2,1,0:T(8,128)(2,1)S(1)}, u32[]{:S(2)}, u32[]{:S(2)}) async-start(bf16[16,4,128,128]{3,2,1,0:T(8,128)(2,1)} %get-tuple-element.14), calls=%async_computation | async-start | bytes 4194304 | tf_op jit(solution)/shard_map/all_to_all | solution.py:296
  105.8 77.9 %all-to-all-start.1 = ((bf16[16,8,2,32,128]{4,3,2,1,0:T(8,128)(2,1)}), bf16[16,8,2,32,128]{4,3,2,1,0:T(8,128)(2,1)S(1)}, u32[]{:S(2)}, u32[]{:S(2)}) async-start(bf16[16,8,2,32,128]{4,3,2,1,0:T(8,128)(2,1)} %shard_map.70), calls=%async_computation.1 | async-start | bytes 4194304 | tf_op jit(solution)/shard_map/all_to_all | solution.py:309
  110.5 36.3 %collective-permute-start.18 = (bf16[4,256,256]{2,1,0:T(8,128)(2,1)S(1)}, bf16[4,256,256]{2,1,0:T(8,128)(2,1)S(1)}, u32[]{:S(2)}, u32[]{:S(2)}) collective-permute-start(bf16[4,256,256]{2,1,0:T(8,128)(2,1)S(1)} %pad_maximum_fusion.1.b0), channel_id=1, source_target_pairs={{3,0},{0,1},{1,2},{2,3},{7,4},{4,5},{5,6},{6,7},{11,8},{8,9},{9,10... | collective-permute-start | bytes 1572872 | tf_op jit(solution)/shard_map/ppermute | solution.py:243
  111.8 46.2 %collective-permute-start.17 = (bf16[4,256,256]{2,1,0:T(8,128)(2,1)S(1)}, bf16[4,256,256]{2,1,0:T(8,128)(2,1)S(1)}, u32[]{:S(2)}, u32[]{:S(2)}) collective-permute-start(bf16[4,256,256]{2,1,0:T(8,128)(2,1)S(1)} %pad_maximum_fusion.1.b0), channel_id=1, source_target_pairs={{2,0},{3,1},{0,2},{1,3},{6,4},{7,5},{4,6},{5,7},{10,8},{11,9},{8,1... | collective-permute-start | bytes 1572872 | tf_op jit(solution)/shard_map/ppermute | solution.py:243
  114.2 43.9 %collective-permute-start.16 = (bf16[4,256,256]{2,1,0:T(8,128)(2,1)S(1)}, bf16[4,256,256]{2,1,0:T(8,128)(2,1)S(1)}, u32[]{:S(2)}, u32[]{:S(2)}) collective-permute-start(bf16[4,256,256]{2,1,0:T(8,128)(2,1)S(1)} %pad_maximum_fusion.1.b0), channel_id=1, source_target_pairs={{1,0},{2,1},{3,2},{0,3},{5,4},{6,5},{7,6},{4,7},{9,8},{10,9},{11,1... | collective-permute-start | bytes 1572872 | tf_op jit(solution)/shard_map/ppermute | solution.py:243
  116.4 65.7 %copy-start.4 = (s32[128,8]{0,1:T(8,128)S(1)}, s32[128,8]{0,1:T(8,128)}, u32[]{:S(2)}) copy-start(s32[128,8]{0,1:T(8,128)} %param.7) | copy-start | bytes 12292
  116.4 41.7 %collective-permute-start.15 = (bf16[4,256,256]{2,1,0:T(8,128)(2,1)S(1)}, bf16[4,256,256]{2,1,0:T(8,128)(2,1)S(1)}, u32[]{:S(2)}, u32[]{:S(2)}) collective-permute-start(bf16[4,256,256]{2,1,0:T(8,128)(2,1)S(1)} %pad_maximum_fusion.a0), channel_id=1, source_target_pairs={{12,0},{0,4},{4,8},{8,12},{13,1},{1,5},{5,9},{9,13},{14,2},{2,6},{... | collective-permute-start | bytes 1572872 | tf_op jit(solution)/shard_map/ppermute | solution.py:243
  117.7 43.3 %collective-permute-start.14 = (bf16[4,256,256]{2,1,0:T(8,128)(2,1)S(1)}, bf16[4,256,256]{2,1,0:T(8,128)(2,1)S(1)}, u32[]{:S(2)}, u32[]{:S(2)}) collective-permute-start(bf16[4,256,256]{2,1,0:T(8,128)(2,1)S(1)} %pad_maximum_fusion.a0), channel_id=1, source_target_pairs={{8,0},{12,4},{0,8},{4,12},{9,1},{13,5},{1,9},{5,13},{10,2},{14,6},... | collective-permute-start | bytes 1572872 | tf_op jit(solution)/shard_map/ppermute | solution.py:243
  146.8 14.2 %collective-permute-start.13 = (bf16[4,256,256]{2,1,0:T(8,128)(2,1)S(1)}, bf16[4,256,256]{2,1,0:T(8,128)(2,1)S(1)}, u32[]{:S(2)}, u32[]{:S(2)}) collective-permute-start(bf16[4,256,256]{2,1,0:T(8,128)(2,1)S(1)} %pad_maximum_fusion.a0), channel_id=1, source_target_pairs={{4,0},{8,4},{12,8},{0,12},{5,1},{9,5},{13,9},{1,13},{6,2},{10,6},{... | collective-permute-start | bytes 1572872 | tf_op jit(solution)/shard_map/ppermute | solution.py:243
  165.6 8.0 %collective-permute-start.21 = (bf16[512,256]{1,0:T(8,128)(2,1)S(1)}, bf16[512,256]{1,0:T(8,128)(2,1)S(1)}, u32[]{:S(2)}, u32[]{:S(2)}) collective-permute-start(bf16[512,256]{1,0:T(8,128)(2,1)S(1)} %shard_map.71.refs_0_), channel_id=1, source_target_pairs={{96,0},{0,32},{32,64},{64,96},{97,1},{1,33},{33,65},{65,97},{98,2}... | collective-permute-start | bytes 786440 | tf_op jit(solution)/shard_map/ppermute | solution.py:243
  166.7 13.3 %collective-permute-start.20 = (bf16[512,256]{1,0:T(8,128)(2,1)S(1)}, bf16[512,256]{1,0:T(8,128)(2,1)S(1)}, u32[]{:S(2)}, u32[]{:S(2)}) collective-permute-start(bf16[512,256]{1,0:T(8,128)(2,1)S(1)} %shard_map.71.refs_0_), channel_id=1, source_target_pairs={{64,0},{96,32},{0,64},{32,96},{65,1},{97,33},{1,65},{33,97},{66,2}... | collective-permute-start | bytes 786440 | tf_op jit(solution)/shard_map/ppermute | solution.py:243
  169.1 12.9 %collective-permute-start.19 = (bf16[512,256]{1,0:T(8,128)(2,1)S(1)}, bf16[512,256]{1,0:T(8,128)(2,1)S(1)}, u32[]{:S(2)}, u32[]{:S(2)}) collective-permute-start(bf16[512,256]{1,0:T(8,128)(2,1)S(1)} %shard_map.71.refs_0_), channel_id=1, source_target_pairs={{32,0},{64,32},{96,64},{0,96},{33,1},{65,33},{97,65},{1,97},{34,2}... | collective-permute-start | bytes 786440 | tf_op jit(solution)/shard_map/ppermute | solution.py:243
  169.2 13.1 %collective-permute-start.22 = (bf16[512,256]{1,0:T(8,128)(2,1)S(1)}, bf16[512,256]{1,0:T(8,128)(2,1)S(1)}, u32[]{:S(2)}, u32[]{:S(2)}) collective-permute-start(bf16[512,256]{1,0:T(8,128)(2,1)S(1)} %shard_map.71.refs_0_), channel_id=1, source_target_pairs={{0,16},{16,0},{1,17},{17,1},{2,18},{18,2},{3,19},{19,3},{4,20},{20... | collective-permute-start | bytes 786440 | tf_op jit(solution)/shard_map/ppermute | solution.py:247
  173.7 8.7 %collective-permute-start.25 = (bf16[512,256]{1,0:T(8,128)(2,1)S(1)}, bf16[512,256]{1,0:T(8,128)(2,1)}, u32[]{:S(2)}, u32[]{:S(2)}) collective-permute-start(bf16[512,256]{1,0:T(8,128)(2,1)S(1)} %collective-permute-done.21.refs_3_), channel_id=1, source_target_pairs={{0,16},{16,0},{1,17},{17,1},{2,18},{18,2},{3,19},{19,3},{4,20},{20... | collective-permute-start | bytes 786440 | tf_op jit(solution)/shard_map/ppermute | solution.py:247
  180.0 3.3 %collective-permute-start.24 = (bf16[512,256]{1,0:T(8,128)(2,1)S(1)}, bf16[512,256]{1,0:T(8,128)(2,1)}, u32[]{:S(2)}, u32[]{:S(2)}) collective-permute-start(bf16[512,256]{1,0:T(8,128)(2,1)S(1)} %collective-permute-done.20.refs_2_), channel_id=1, source_target_pairs={{0,16},{16,0},{1,17},{17,1},{2,18},{18,2},{3,19},{19,3},{4,20},{20... | collective-permute-start | bytes 786440 | tf_op jit(solution)/shard_map/ppermute | solution.py:247
  182.0 1.7 collective-permute-start.23
